TPU v7x, 64 devices: a 2x2x8 block of a 4x4x8 slice. The times are simulated.
64 devices in a mesh: rep: 8 (over x, y, core), dp: 8 (over z).
Axes of the slice: x: 2, y: 2, z: 8, core: 2. Of those that a mesh axis runs over, the one named last changes fastest.
The devices are a block of a 4x4x8 slice.
Arguments:
- x: bfloat16 [64, 4096, 512], P(('rep', 'dp')), parts along dimension 0
- dy: bfloat16 [64, 4096, 512], P(('rep', 'dp')), parts along dimension 0
- w_gate: bfloat16 [2, 512, 1792], replicated
- w_up: bfloat16 [2, 512, 1792], replicated
- w_down: bfloat16 [2, 1792, 512], replicated
- m_w_gate: float32 [2, 512, 1792], P(None, 'dp')
- m_w_up: float32 [2, 512, 1792], P(None, 'dp')
- m_w_down: float32 [2, 1792, 512], P(None, 'dp')
- v_w_gate: float32 [2, 512, 1792], P(None, 'dp')
- v_w_up: float32 [2, 512, 1792], P(None, 'dp')
- v_w_down: float32 [2, 1792, 512], P(None, 'dp')
Outputs:
- output 1: bfloat16 [16, 512, 1792], P('rep'), parts along dimension 0
- output 2: bfloat16 [16, 512, 1792], P('rep'), parts along dimension 0
- output 3: bfloat16 [16, 1792, 512], P('rep'), parts along dimension 0
- output 4: float32 [16, 512, 1792], P('rep', 'dp'), parts along dimension 0
- output 5: float32 [16, 512, 1792], P('rep', 'dp'), parts along dimension 0
- output 6: float32 [16, 1792, 512], P('rep', 'dp'), parts along dimension 0
- output 7: float32 [16, 512, 1792], P('rep', 'dp'), parts along dimension 0
- output 8: float32 [16, 512, 1792], P('rep', 'dp'), parts along dimension 0
- output 9: float32 [16, 1792, 512], P('rep', 'dp'), parts along dimension 0
There are 8 independent parts. A program takes and returns all parts, laid end to end along the dimension named above; an argument that names none is the same for every part.
All inputs are finite; a program needn't handle non-finite values.
Results may differ from a plain program's by a relative error of at most 0.0204.
Values are sent between devices in bfloat16 or wider.
A program may use at most 768 MiB of HBM per device.

v0:
```python
import jax
import jax.numpy as jnp
from jax import lax

NAMES = ("w_gate", "w_up", "w_down")


def matmul(a, w):
    return jnp.dot(a, w, preferred_element_type=jnp.float32).astype(jnp.bfloat16)


def normed(h):
    wide = h.astype(jnp.float32)
    scale = lax.rsqrt(jnp.mean(wide**2, -1, keepdims=True) + 1e-6)
    return (wide * scale).astype(jnp.bfloat16)


def layer(h, w):
    a = normed(h)
    gate = jnp.dot(a, w["w_gate"], preferred_element_type=jnp.float32)
    up = jnp.dot(a, w["w_up"], preferred_element_type=jnp.float32)
    return h + matmul((jax.nn.silu(gate) * up).astype(jnp.bfloat16), w["w_down"])


def adamw(w, m, v, g):
    m = 0.9 * m + 0.1 * g
    v = 0.95 * v + 0.05 * g * g
    step = m * lax.rsqrt(v + 1e-8) + 0.1 * w
    return (w - 0.02 * step).astype(jnp.bfloat16), m, v


def stack(weights, h):
    for number in range(weights["w_gate"].shape[0]):
        h = layer(h, {name: w[number] for name, w in weights.items()})
    return h


def solution(mesh):
    groups = mesh.shape["rep"]

    def step(x, dy, *arrays):
        weights, m, v = (arrays[i : i + 3] for i in (0, 3, 6))
        x, dy = (t.reshape(groups, -1, *t.shape[1:]) for t in (x, dy))

        def of_a_group(x, dy):
            _, back = jax.vjp(lambda w: stack(w, x), dict(zip(NAMES, weights, strict=True)))
            by_weights = back(dy)[0]
            gradients = [by_weights[name].astype(jnp.float32) for name in NAMES]
            new = [adamw(w.astype(jnp.float32), m, v, g) for w, m, v, g in zip(weights, m, v, gradients, strict=True)]
            return tuple(one[which] for which in range(3) for one in new)

        return tuple(t.reshape(-1, *t.shape[2:]) for t in jax.vmap(of_a_group)(x, dy))

    return step
```

profile of v0, /device:TPU:22, one launch (start us, length us, event | category | flops | bytes accessed | tf_op | source)
XLA Modules:
  0.0 789.6 jit_solution(16963302706158296101)
XLA Ops:
  10.3 6.4 copy
  16.7 6.4 copy.1
  23.1 13.3 %convolution_convert_fusion.1 = bf16[4096,1792]{1,0:T(8,128)(2,1)} fusion(bf16[1,4096,512]{2,1,0:T(8,128)(2,1)} %param.17, bf16[2,1792,512]{2,1,0:T(8,128)(2,1)} %param.16), kind=kOutput, calls=%fused_computation.199 | convolution fusion | flops 7523532800 | bytes 20709376 | tf_op jit(solution)/vmap(transpose(jvp()))/dot_general | solution.py:9
  36.5 13.5 %fusion.215 = f32[4096,1792]{1,0:T(8,128)} fusion(bf16[2,512,1792]{2,1,0:T(8,128)(2,1)S(1)} %copy-done.25, bf16[1,4096,512]{2,1,0:T(8,128)(2,1)S(1)} %copy-done.6, f32[4096]{0:T(1024)S(1)} %add_rsqrt_fusion), kind=kOutput, calls=%fused_computation.241 | convolution fusion | flops 7522484224 | bytes 35405824 | tf_op jit(solution)/vmap(jvp())/dot_general | solution.py:20
  50.0 29.1 %fusion.164 = (bf16[1,1,4096,1792]{3,2,1,0:T(8,128)(2,1)}, f32[4096,1792]{1,0:T(8,128)}) fusion(f32[4096,1792]{1,0:T(8,128)} %fusion.215, bf16[2,512,1792]{2,1,0:T(8,128)(2,1)} %param.15, bf16[1,4096,512]{2,1,0:T(8,128)(2,1)} %param.14, f32[4096]{0:T(1024)S(1)} %add_rsqrt_fusion), kind=kOutput, calls=%fused_computation.191 | convolution fusion | flops 7566524416 | bytes 79446016 | tf_op jit(solution)/vmap(jvp())/dot_general | solution.py:21
  79.1 13.1 %fusion.174 = (f32[4096]{0:T(1024)S(1)}, bf16[1,1,4096,512]{2,3,1,0:T(8,128)(2,1)S(1)}) fusion(bf16[2,1792,512]{2,1,0:T(8,128)(2,1)} %param.16, bf16[1,1,4096,1792]{3,2,1,0:T(8,128)(2,1)} %get-tuple-element.263, bf16[1,4096,512]{1,2,0:T(8,128)(2,1)} %copy), kind=kOutput, calls=%fused_computation.213 | convolution fusion | flops 7526674432 | bytes 24920064 | tf_op jit(solution)/vmap(jvp())/dot_general | solution.py:9
  97.3 13.6 %fusion.203 = f32[4096,1792]{1,0:T(8,128)} fusion(bf16[1,1,4096,512]{2,3,1,0:T(8,128)(2,1)S(1)} %fusion.175, bf16[2,512,1792]{2,1,0:T(8,128)(2,1)S(1)} %copy-done.24), kind=kOutput, calls=%fused_computation.229 | convolution fusion | flops 7516192768 | bytes 35389440 | tf_op jit(solution)/vmap(jvp())/dot_general | solution.py:21
  110.9 41.0 %fusion.153 = (bf16[1,1,4096,1792]{3,2,1,0:T(8,128)(2,1)}, bf16[1,1,4096,1792]{3,2,1,0:T(8,128)(2,1)}, f32[4096,1792]{1,0:T(8,128)}) fusion(f32[4096,1792]{1,0:T(8,128)} %fusion.203, bf16[4096,1792]{1,0:T(8,128)(2,1)} %convolution_convert_fusion.1, bf16[2,512,1792]{2,1,0:T(8,128)(2,1)} %param.12, bf16[1,1,4096,512]{2,3,1,0:T(8,128)(2,1)} %copy-done), kind=kOutput, calls=%fused_computation.175 | convolution fusion | flops 7626293248 | bytes 108789760 | tf_op jit(solution)/vmap(jvp())/dot_general | solution.py:20
  151.9 25.3 %fusion.163 = bf16[1,1,4096,1792]{3,2,1,0:T(8,128)(2,1)} fusion(f32[4096,1792]{1,0:T(8,128)} %fusion.203, f32[4096,1792]{1,0:T(8,128)} %get-tuple-element.267), kind=kLoop, calls=%fused_computation.189 | loop fusion | flops 44040192 | bytes 73400320 | tf_op jit(solution)/vmap(jvp())/convert_element_type | solution.py:22
  177.2 19.0 %copy.2 = bf16[1,1,4096,1792]{2,3,1,0:T(8,128)(2,1)} copy(bf16[1,1,4096,1792]{3,2,1,0:T(8,128)(2,1)} %fusion.163) | data formatting | bytes 29360128
  196.2 6.5 copy.3
  202.7 58.0 %while.16 = (bf16[1,1,4096,1792]{2,3,1,0:T(8,128)(2,1)}, bf16[1,1,4096,512]{3,2,1,0:T(8,128)(2,1)}, f32[1,224,512]{2,1,0:T(8,128)S(1)}, f32[1,224,512]{2,1,0:T(8...) while((bf16[1,1,4096,1792]{2,3,1,0:T(8,128)(2,1)}, ...), condition=%wide.windowed_dot_general_cond_rs.4.clone, body=%wide.windowed_dot_general_body_rs.4.clone.sunk | while | flops 3773464576 | bytes 129761952 | solution.py:9
  205.0 5.3 collective-permute-start.17
  212.8 5.5 fusion.345
  226.3 7.7 collective-permute-done.18
  242.0 5.5 fusion.345
  253.8 6.0 collective-permute-done.18
  261.4 19.1 %copy.4 = bf16[1,1,4096,1792]{2,3,1,0:T(8,128)(2,1)} copy(bf16[1,1,4096,1792]{3,2,1,0:T(8,128)(2,1)} %get-tuple-element.263) | data formatting | bytes 29360128
  280.5 14.9 %fusion.180 = bf16[4096,512]{0,1:T(8,128)(2,1)} fusion(bf16[1,1,4096,1792]{3,2,1,0:T(8,128)(2,1)} %get-tuple-element.622, bf16[2,512,1792]{2,1,0:T(8,128)(2,1)} %param.15), kind=kOutput, calls=%fused_computation.218 | convolution fusion | flops 7516192768 | bytes 20709376 | tf_op jit(solution)/vmap(transpose(jvp()))/dot_general | solution.py:21
  295.5 12.8 %fusion.176 = (f32[4096]{0:T(1024)S(1)}, bf16[1,1,4096,512]{2,3,1,0:T(8,128)(2,1)S(1)}) fusion(bf16[1,1,4096,512]{2,3,1,0:T(8,128)(2,1)S(1)} %copy-done.8, bf16[4096,512]{0,1:T(8,128)(2,1)} %fusion.180, bf16[2,512,1792]{2,1,0:T(8,128)(2,1)} %param.12, bf16[1,1,4096,1792]{3,2,1,0:T(8,128)(2,1)} %get-tuple-element.544), kind=kOutput, calls=%fused_computation.215 | convolution fusion | flops 7526674432 | bytes 29114368 | tf_op jit(solution)/vmap(transpose(jvp()))/dot_general | solution.py:20
  308.3 4.2 fusion.198
  312.6 6.5 copy.5
  319.0 48.0 %while.17 = (bf16[1,1,4096,1792]{2,3,1,0:T(8,128)(2,1)}, bf16[1,1,4096,512]{3,2,1,0:T(8,128)(2,1)}, f32[1,224,512]{2,1,0:T(8,128)S(1)}, f32[1,224,512]{2,1,0:T(8...) while((bf16[1,1,4096,1792]{2,3,1,0:T(8,128)(2,1)}, ...), condition=%wide.windowed_dot_general_cond_rs.5.clone, body=%wide.windowed_dot_general_body_rs.5.clone.sunk | while | flops 3773464576 | bytes 129761952 | solution.py:9
  325.1 5.5 fusion.353
  336.2 4.4 collective-permute-done.22
  348.6 5.5 fusion.353
  359.7 6.2 collective-permute-done.22
  369.8 62.1 %while.14 = (bf16[1,1,4096,512]{2,3,1,0:T(8,128)(2,1)}, bf16[1,1,4096,1792]{3,2,1,0:T(8,128)(2,1)}, f32[1,64,1792]{2,1,0:T(8,128)S(1)}, f32[1,64,1792]{2,1,0:T(8...) while((bf16[1,1,4096,512]{2,3,1,0:T(8,128)(2,1)}, ...), condition=%wide.windowed_dot_general_cond_rs.2.clone, body=%wide.windowed_dot_general_body_rs.2.clone.sunk | while | flops 3762978816 | bytes 54264420 | solution.py:21
  375.6 7.6 fusion.329
  383.8 3.4 collective-permute-done.8
  390.6 7.6 fusion.331
  408.9 7.6 fusion.329
  420.8 7.6 fusion.331
  431.9 5.4 multiply_convert_fusion
  437.3 36.0 %convert_multiply_fusion = (bf16[1,1,4096,1792]{3,2,1,0:T(8,128)(2,1)}, bf16[1,1,4096,1792]{3,2,1,0:T(8,128)(2,1)}) fusion(f32[4096,1792]{1,0:T(8,128)} %fusion.215, f32[4096,1792]{1,0:T(8,128)} %get-tuple-element.264, bf16[2,1792,512]{2,1,0:T(8,128)(2,1)} %param.16, bf16[1,1,4096,512]{2,3,1,0:T(8,128)(2,1)} %fusion.198), kind=kOutput, calls=%fused_computation.170 | convolution fusion | flops 7633633280 | bytes 94109696 | tf_op jit(solution)/vmap(transpose(jvp()))/dot_general | solution.py:9
  473.3 61.8 %while.15 = (bf16[1,1,4096,512]{2,3,1,0:T(8,128)(2,1)}, bf16[1,1,4096,1792]{3,2,1,0:T(8,128)(2,1)}, f32[1,64,1792]{2,1,0:T(8,128)S(1)}, f32[1,64,1792]{2,1,0:T(8...) while((bf16[1,1,4096,512]{2,3,1,0:T(8,128)(2,1)}, ...), condition=%wide.windowed_dot_general_cond_rs.3.clone, body=%wide.windowed_dot_general_body_rs.3.clone.sunk | while | flops 3762978816 | bytes 54264420 | solution.py:21
  478.7 7.6 fusion.337
  493.2 7.6 fusion.339
  512.2 7.6 fusion.337
  525.6 7.6 fusion.339
  540.4 3.5 fusion.252
  544.0 83.7 %while.12 = (bf16[1,1,4096,512]{2,3,1,0:T(8,128)(2,1)}, bf16[1,1,4096,1792]{3,2,1,0:T(8,128)(2,1)}, f32[1,64,1792]{2,1,0:T(8,128)S(1)}, f32[1,64,1792]{2,1,0:T(8...) while((bf16[1,1,4096,512]{2,3,1,0:T(8,128)(2,1)}, ...), condition=%wide.windowed_dot_general_cond_rs.clone, body=%wide.windowed_dot_general_body_rs.clone.sunk | while | flops 3762978816 | bytes 54264420 | solution.py:20
  549.6 7.6 fusion.313
  564.6 3.7 collective-permute-start.3
  568.3 7.6 fusion.315
  575.9 11.6 %collective-permute-done.2 = f32[1,64,1792]{2,1,0:T(8,128)S(1)} collective-permute-done((f32[1,64,1792]{2,1,0:T(8,128)}, f32[1,64,1792]{2,1,0:T(8,128)S(1)}, u32[]{:S(2)}, u32[]{:S(2)}) %collective-permute-start.2) | collective-permute-done | bytes 458784 | tf_op jit(solution)/vmap(transpose(jvp()))/dot_general | solution.py:20
  590.6 3.4 collective-permute-start.1
  595.9 7.6 fusion.313
  604.1 7.7 collective-permute-done
  616.9 7.6 fusion.315
  631.4 3.4 fusion.253
  634.9 81.7 %while.13 = (bf16[1,1,4096,512]{2,3,1,0:T(8,128)(2,1)}, bf16[1,1,4096,1792]{3,2,1,0:T(8,128)(2,1)}, f32[1,64,1792]{2,1,0:T(8,128)S(1)}, f32[1,64,1792]{2,1,0:T(8...) while((bf16[1,1,4096,512]{2,3,1,0:T(8,128)(2,1)}, ...), condition=%wide.windowed_dot_general_cond_rs.1.clone, body=%wide.windowed_dot_general_body_rs.1.clone.sunk | while | flops 3762978816 | bytes 54264420 | solution.py:20
  640.3 7.6 fusion.321
  649.6 4.8 collective-permute-done.5
  655.2 3.6 collective-permute-start.6
  658.8 7.6 fusion.323
  666.4 13.1 %collective-permute-done.6 = f32[1,64,1792]{2,1,0:T(8,128)S(1)} collective-permute-done((f32[1,64,1792]{2,1,0:T(8,128)}, f32[1,64,1792]{2,1,0:T(8,128)S(1)}, u32[]{:S(2)}, u32[]{:S(2)}) %collective-permute-start.6) | collective-permute-done | bytes 458784 | tf_op jit(solution)/vmap(transpose(jvp()))/dot_general | solution.py:20
  688.5 7.6 fusion.321
  696.7 7.1 collective-permute-done.4
  707.9 7.6 fusion.323
  717.8 8.6 %collective-permute-done.25 = f32[1,64,1792]{2,1,0:T(8,128)S(1)} collective-permute-done((f32[1,64,1792]{2,1,0:T(8,128)S(1)}, f32[1,64,1792]{2,1,0:T(8,128)S(1)}, u32[]{:S(2)}, u32[]{:S(2)}) %collective-permute-start.25) | collective-permute-done | bytes 458784 | tf_op jit(solution)/vmap(transpose(jvp()))/dot_general | solution.py:20
  726.4 3.4 fusion.254
  730.0 44.8 %all-gather.10.cloned.1.call-done = bf16[1,2,512,1792]{3,2,1,0:T(8,128)(2,1)} async-done(((bf16[1,2,64,1792]{3,2,1,0:T(8,128)(2,1)}), bf16[1,2,512,1792]{3,2,1,0:T(8,128)(2,1)}) %all-gather.10.cloned.1.call-update) | async-done | bytes 3670032 | tf_op jit(solution)/reshape | solution.py:52
  774.8 4.3 copy.63
  (254 shorter events, 164.9 us)
Async XLA Ops:
  7.2 722.8 %all-gather.14.cloned.1.call-start = ((), (), s32[]{:S(2)}) async-start(), calls=%async_computation.2 | async-start | bytes 4128768 | tf_op jit(solution)/reshape | solution.py:52
  16.7 33.3 %copy-start.22 = (f32[4096]{0:T(1024)}, f32[4096]{0:T(1024)S(1)}, u32[]{:S(2)}) copy-start(f32[4096]{0:T(1024)S(1)} %add_rsqrt_fusion) | copy-start | bytes 49156
  202.7 18.0 %collective-permute-start.16 = (f32[1,224,512]{2,1,0:T(8,128)S(1)}, f32[1,224,512]{2,1,0:T(8,128)S(1)}, u32[]{:S(2)}, u32[]{:S(2)}) collective-permute-start(f32[1,224,512]{2,1,0:T(8,128)S(1)} %broadcast_select_fusion.32), channel_id=29, source_target_pairs={{0,1},{1,2},{2,3},{3,4},{4,5},{5,6},{6,7},{7,0},{8,9},{9,10},{10,1... | collective-permute-start | bytes 1376264 | tf_op jit(solution)/vmap(transpose(jvp()))/dot_general | solution.py:9
  205.0 15.7 %collective-permute-start.17 = (f32[1,224,512]{2,1,0:T(8,128)S(1)}, f32[1,224,512]{2,1,0:T(8,128)S(1)}, u32[]{:S(2)}, u32[]{:S(2)}) collective-permute-start(f32[1,224,512]{2,1,0:T(8,128)S(1)} %broadcast_select_fusion.33), channel_id=28, source_target_pairs={{0,7},{1,0},{2,1},{3,2},{4,3},{5,4},{6,5},{7,6},{8,15},{9,8},{10,9... | collective-permute-start | bytes 1376264 | tf_op jit(solution)/vmap(transpose(jvp()))/dot_general | solution.py:9
  220.9 13.1 %collective-permute-start.18 = (f32[1,224,512]{2,1,0:T(8,128)S(1)}, f32[1,224,512]{2,1,0:T(8,128)S(1)}, u32[]{:S(2)}, u32[]{:S(2)}) collective-permute-start(f32[1,224,512]{2,1,0:T(8,128)S(1)} %get-tuple-element.491), channel_id=31, source_target_pairs={{0,1},{1,2},{2,3},{3,4},{4,5},{5,6},{6,7},{7,0},{8,9},{9,10},{10,1... | collective-permute-start | bytes 1376264 | tf_op jit(solution)/vmap(transpose(jvp()))/dot_general | solution.py:9
  221.0 13.0 %collective-permute-start.19 = (f32[1,224,512]{2,1,0:T(8,128)S(1)}, f32[1,224,512]{2,1,0:T(8,128)S(1)}, u32[]{:S(2)}, u32[]{:S(2)}) collective-permute-start(f32[1,224,512]{2,1,0:T(8,128)S(1)} %get-tuple-element.492), channel_id=30, source_target_pairs={{0,7},{1,0},{2,1},{3,2},{4,3},{5,4},{6,5},{7,6},{8,15},{9,8},{10,9... | collective-permute-start | bytes 1376264 | tf_op jit(solution)/vmap(transpose(jvp()))/dot_general | solution.py:9
  236.0 12.2 %collective-permute-start.16 = (f32[1,224,512]{2,1,0:T(8,128)S(1)}, f32[1,224,512]{2,1,0:T(8,128)S(1)}, u32[]{:S(2)}, u32[]{:S(2)}) collective-permute-start(f32[1,224,512]{2,1,0:T(8,128)S(1)} %broadcast_select_fusion.32), channel_id=29, source_target_pairs={{0,1},{1,2},{2,3},{3,4},{4,5},{5,6},{6,7},{7,0},{8,9},{9,10},{10,1... | collective-permute-start | bytes 1376264 | tf_op jit(solution)/vmap(transpose(jvp()))/dot_general | solution.py:9
  237.5 10.8 %collective-permute-start.17 = (f32[1,224,512]{2,1,0:T(8,128)S(1)}, f32[1,224,512]{2,1,0:T(8,128)S(1)}, u32[]{:S(2)}, u32[]{:S(2)}) collective-permute-start(f32[1,224,512]{2,1,0:T(8,128)S(1)} %broadcast_select_fusion.33), channel_id=28, source_target_pairs={{0,7},{1,0},{2,1},{3,2},{4,3},{5,4},{6,5},{7,6},{8,15},{9,8},{10,9... | collective-permute-start | bytes 1376264 | tf_op jit(solution)/vmap(transpose(jvp()))/dot_general | solution.py:9
  248.4 11.4 %collective-permute-start.18 = (f32[1,224,512]{2,1,0:T(8,128)S(1)}, f32[1,224,512]{2,1,0:T(8,128)S(1)}, u32[]{:S(2)}, u32[]{:S(2)}) collective-permute-start(f32[1,224,512]{2,1,0:T(8,128)S(1)} %get-tuple-element.491), channel_id=31, source_target_pairs={{0,1},{1,2},{2,3},{3,4},{4,5},{5,6},{6,7},{7,0},{8,9},{9,10},{10,1... | collective-permute-start | bytes 1376264 | tf_op jit(solution)/vmap(transpose(jvp()))/dot_general | solution.py:9
  249.5 10.3 %collective-permute-start.19 = (f32[1,224,512]{2,1,0:T(8,128)S(1)}, f32[1,224,512]{2,1,0:T(8,128)S(1)}, u32[]{:S(2)}, u32[]{:S(2)}) collective-permute-start(f32[1,224,512]{2,1,0:T(8,128)S(1)} %get-tuple-element.492), channel_id=30, source_target_pairs={{0,7},{1,0},{2,1},{3,2},{4,3},{5,4},{6,5},{7,6},{8,15},{9,8},{10,9... | collective-permute-start | bytes 1376264 | tf_op jit(solution)/vmap(transpose(jvp()))/dot_general | solution.py:9
  260.7 19.8 %copy-start.10 = (f32[1,224,512]{2,1,0:T(8,128)}, f32[1,224,512]{2,1,0:T(8,128)S(1)}, u32[]{:S(2)}) copy-start(f32[1,224,512]{2,1,0:T(8,128)S(1)} %get-tuple-element.44) | copy-start | bytes 1376260
  260.7 277.4 %collective-permute-start.28 = (f32[1,224,512]{2,1,0:T(8,128)}, f32[1,224,512]{2,1,0:T(8,128)}, u32[]{:S(2)}, u32[]{:S(2)}) collective-permute-start(f32[1,224,512]{2,1,0:T(8,128)} %get-tuple-element.45), channel_id=32, source_target_pairs={{0,1},{1,2},{2,3},{3,4},{4,5},{5,6},{6,7},{7,0},{8,9},{9,10},{10,1... | collective-permute-start | bytes 1376264 | tf_op jit(solution)/vmap(transpose(jvp()))/dot_general | solution.py:9
  319.1 11.5 %collective-permute-start.20 = (f32[1,224,512]{2,1,0:T(8,128)S(1)}, f32[1,224,512]{2,1,0:T(8,128)S(1)}, u32[]{:S(2)}, u32[]{:S(2)}) collective-permute-start(f32[1,224,512]{2,1,0:T(8,128)S(1)} %broadcast_select_fusion.34), channel_id=35, source_target_pairs={{0,1},{1,2},{2,3},{3,4},{4,5},{5,6},{6,7},{7,0},{8,9},{9,10},{10,1... | collective-permute-start | bytes 1376264 | tf_op jit(solution)/vmap(transpose(jvp()))/dot_general | solution.py:9
  320.9 9.7 %collective-permute-start.21 = (f32[1,224,512]{2,1,0:T(8,128)S(1)}, f32[1,224,512]{2,1,0:T(8,128)S(1)}, u32[]{:S(2)}, u32[]{:S(2)}) collective-permute-start(f32[1,224,512]{2,1,0:T(8,128)S(1)} %broadcast_select_fusion.35), channel_id=34, source_target_pairs={{0,7},{1,0},{2,1},{3,2},{4,3},{5,4},{6,5},{7,6},{8,15},{9,8},{10,9... | collective-permute-start | bytes 1376264 | tf_op jit(solution)/vmap(transpose(jvp()))/dot_general | solution.py:9
  330.8 9.8 %collective-permute-start.22 = (f32[1,224,512]{2,1,0:T(8,128)S(1)}, f32[1,224,512]{2,1,0:T(8,128)S(1)}, u32[]{:S(2)}, u32[]{:S(2)}) collective-permute-start(f32[1,224,512]{2,1,0:T(8,128)S(1)} %get-tuple-element.500), channel_id=37, source_target_pairs={{0,1},{1,2},{2,3},{3,4},{4,5},{5,6},{6,7},{7,0},{8,9},{9,10},{10,1... | collective-permute-start | bytes 1376264 | tf_op jit(solution)/vmap(transpose(jvp()))/dot_general | solution.py:9
  331.9 8.7 %collective-permute-start.23 = (f32[1,224,512]{2,1,0:T(8,128)S(1)}, f32[1,224,512]{2,1,0:T(8,128)S(1)}, u32[]{:S(2)}, u32[]{:S(2)}) collective-permute-start(f32[1,224,512]{2,1,0:T(8,128)S(1)} %get-tuple-element.501), channel_id=36, source_target_pairs={{0,7},{1,0},{2,1},{3,2},{4,3},{5,4},{6,5},{7,6},{8,15},{9,8},{10,9... | collective-permute-start | bytes 1376264 | tf_op jit(solution)/vmap(transpose(jvp()))/dot_general | solution.py:9
  342.6 11.6 %collective-permute-start.20 = (f32[1,224,512]{2,1,0:T(8,128)S(1)}, f32[1,224,512]{2,1,0:T(8,128)S(1)}, u32[]{:S(2)}, u32[]{:S(2)}) collective-permute-start(f32[1,224,512]{2,1,0:T(8,128)S(1)} %broadcast_select_fusion.34), channel_id=35, source_target_pairs={{0,1},{1,2},{2,3},{3,4},{4,5},{5,6},{6,7},{7,0},{8,9},{9,10},{10,1... | collective-permute-start | bytes 1376264 | tf_op jit(solution)/vmap(transpose(jvp()))/dot_general | solution.py:9
  343.7 10.5 %collective-permute-start.21 = (f32[1,224,512]{2,1,0:T(8,128)S(1)}, f32[1,224,512]{2,1,0:T(8,128)S(1)}, u32[]{:S(2)}, u32[]{:S(2)}) collective-permute-start(f32[1,224,512]{2,1,0:T(8,128)S(1)} %broadcast_select_fusion.35), channel_id=34, source_target_pairs={{0,7},{1,0},{2,1},{3,2},{4,3},{5,4},{6,5},{7,6},{8,15},{9,8},{10,9... | collective-permute-start | bytes 1376264 | tf_op jit(solution)/vmap(transpose(jvp()))/dot_general | solution.py:9
  354.3 11.6 %collective-permute-start.22 = (f32[1,224,512]{2,1,0:T(8,128)S(1)}, f32[1,224,512]{2,1,0:T(8,128)S(1)}, u32[]{:S(2)}, u32[]{:S(2)}) collective-permute-start(f32[1,224,512]{2,1,0:T(8,128)S(1)} %get-tuple-element.500), channel_id=37, source_target_pairs={{0,1},{1,2},{2,3},{3,4},{4,5},{5,6},{6,7},{7,0},{8,9},{9,10},{10,1... | collective-permute-start | bytes 1376264 | tf_op jit(solution)/vmap(transpose(jvp()))/dot_general | solution.py:9
  356.6 9.4 %collective-permute-start.23 = (f32[1,224,512]{2,1,0:T(8,128)S(1)}, f32[1,224,512]{2,1,0:T(8,128)S(1)}, u32[]{:S(2)}, u32[]{:S(2)}) collective-permute-start(f32[1,224,512]{2,1,0:T(8,128)S(1)} %get-tuple-element.501), channel_id=36, source_target_pairs={{0,7},{1,0},{2,1},{3,2},{4,3},{5,4},{6,5},{7,6},{8,15},{9,8},{10,9... | collective-permute-start | bytes 1376264 | tf_op jit(solution)/vmap(transpose(jvp()))/dot_general | solution.py:9
  367.0 172.3 %collective-permute-start.29 = (f32[1,224,512]{2,1,0:T(8,128)}, f32[1,224,512]{2,1,0:T(8,128)}, u32[]{:S(2)}, u32[]{:S(2)}) collective-permute-start(f32[1,224,512]{2,1,0:T(8,128)} %get-tuple-element.47), channel_id=38, source_target_pairs={{0,1},{1,2},{2,3},{3,4},{4,5},{5,6},{6,7},{7,0},{8,9},{9,10},{10,1... | collective-permute-start | bytes 1376264 | tf_op jit(solution)/vmap(transpose(jvp()))/dot_general | solution.py:9
  369.8 62.1 %copy-start.23 = (f32[4096]{0:T(1024)S(1)}, f32[4096]{0:T(1024)}, u32[]{:S(2)}) copy-start(f32[4096]{0:T(1024)} %copy-done.22) | copy-start | bytes 49156
  370.2 17.0 %collective-permute-start.8 = (f32[1,64,1792]{2,1,0:T(8,128)S(1)}, f32[1,64,1792]{2,1,0:T(8,128)S(1)}, u32[]{:S(2)}, u32[]{:S(2)}) collective-permute-start(f32[1,64,1792]{2,1,0:T(8,128)S(1)} %broadcast_select_fusion.28), channel_id=16, source_target_pairs={{0,1},{1,2},{2,3},{3,4},{4,5},{5,6},{6,7},{7,0},{8,9},{9,10},{10,1... | collective-permute-start | bytes 1376264 | tf_op jit(solution)/vmap(transpose(jvp()))/dot_general | solution.py:21
  371.7 15.5 %collective-permute-start.9 = (f32[1,64,1792]{2,1,0:T(8,128)S(1)}, f32[1,64,1792]{2,1,0:T(8,128)S(1)}, u32[]{:S(2)}, u32[]{:S(2)}) collective-permute-start(f32[1,64,1792]{2,1,0:T(8,128)S(1)} %broadcast_select_fusion.29), channel_id=15, source_target_pairs={{0,7},{1,0},{2,1},{3,2},{4,3},{5,4},{6,5},{7,6},{8,15},{9,8},{10,9... | collective-permute-start | bytes 1376264 | tf_op jit(solution)/vmap(transpose(jvp()))/dot_general | solution.py:21
  387.3 12.5 %collective-permute-start.10 = (f32[1,64,1792]{2,1,0:T(8,128)S(1)}, f32[1,64,1792]{2,1,0:T(8,128)S(1)}, u32[]{:S(2)}, u32[]{:S(2)}) collective-permute-start(f32[1,64,1792]{2,1,0:T(8,128)S(1)} %get-tuple-element.473), channel_id=18, source_target_pairs={{0,1},{1,2},{2,3},{3,4},{4,5},{5,6},{6,7},{7,0},{8,9},{9,10},{10,1... | collective-permute-start | bytes 1376264 | tf_op jit(solution)/vmap(transpose(jvp()))/dot_general | solution.py:21
  389.6 12.0 %collective-permute-start.11 = (f32[1,64,1792]{2,1,0:T(8,128)S(1)}, f32[1,64,1792]{2,1,0:T(8,128)S(1)}, u32[]{:S(2)}, u32[]{:S(2)}) collective-permute-start(f32[1,64,1792]{2,1,0:T(8,128)S(1)} %get-tuple-element.474), channel_id=17, source_target_pairs={{0,7},{1,0},{2,1},{3,2},{4,3},{5,4},{6,5},{7,6},{8,15},{9,8},{10,9... | collective-permute-start | bytes 1376264 | tf_op jit(solution)/vmap(transpose(jvp()))/dot_general | solution.py:21
  403.5 13.8 %collective-permute-start.8 = (f32[1,64,1792]{2,1,0:T(8,128)S(1)}, f32[1,64,1792]{2,1,0:T(8,128)S(1)}, u32[]{:S(2)}, u32[]{:S(2)}) collective-permute-start(f32[1,64,1792]{2,1,0:T(8,128)S(1)} %broadcast_select_fusion.28), channel_id=16, source_target_pairs={{0,1},{1,2},{2,3},{3,4},{4,5},{5,6},{6,7},{7,0},{8,9},{9,10},{10,1... | collective-permute-start | bytes 1376264 | tf_op jit(solution)/vmap(transpose(jvp()))/dot_general | solution.py:21
  405.9 11.4 %collective-permute-start.9 = (f32[1,64,1792]{2,1,0:T(8,128)S(1)}, f32[1,64,1792]{2,1,0:T(8,128)S(1)}, u32[]{:S(2)}, u32[]{:S(2)}) collective-permute-start(f32[1,64,1792]{2,1,0:T(8,128)S(1)} %broadcast_select_fusion.29), channel_id=15, source_target_pairs={{0,7},{1,0},{2,1},{3,2},{4,3},{5,4},{6,5},{7,6},{8,15},{9,8},{10,9... | collective-permute-start | bytes 1376264 | tf_op jit(solution)/vmap(transpose(jvp()))/dot_general | solution.py:21
  417.4 13.6 %collective-permute-start.10 = (f32[1,64,1792]{2,1,0:T(8,128)S(1)}, f32[1,64,1792]{2,1,0:T(8,128)S(1)}, u32[]{:S(2)}, u32[]{:S(2)}) collective-permute-start(f32[1,64,1792]{2,1,0:T(8,128)S(1)} %get-tuple-element.473), channel_id=18, source_target_pairs={{0,1},{1,2},{2,3},{3,4},{4,5},{5,6},{6,7},{7,0},{8,9},{9,10},{10,1... | collective-permute-start | bytes 1376264 | tf_op jit(solution)/vmap(transpose(jvp()))/dot_general | solution.py:21
  418.4 12.7 %collective-permute-start.11 = (f32[1,64,1792]{2,1,0:T(8,128)S(1)}, f32[1,64,1792]{2,1,0:T(8,128)S(1)}, u32[]{:S(2)}, u32[]{:S(2)}) collective-permute-start(f32[1,64,1792]{2,1,0:T(8,128)S(1)} %get-tuple-element.474), channel_id=17, source_target_pairs={{0,7},{1,0},{2,1},{3,2},{4,3},{5,4},{6,5},{7,6},{8,15},{9,8},{10,9... | collective-permute-start | bytes 1376264 | tf_op jit(solution)/vmap(transpose(jvp()))/dot_general | solution.py:21
  431.9 41.4 %copy-start.14 = (f32[1,64,1792]{2,1,0:T(8,128)}, f32[1,64,1792]{2,1,0:T(8,128)S(1)}, u32[]{:S(2)}) copy-start(f32[1,64,1792]{2,1,0:T(8,128)S(1)} %get-tuple-element.40) | copy-start | bytes 1376260
  431.9 197.3 %collective-permute-start.26 = (f32[1,64,1792]{2,1,0:T(8,128)}, f32[1,64,1792]{2,1,0:T(8,128)}, u32[]{:S(2)}, u32[]{:S(2)}) collective-permute-start(f32[1,64,1792]{2,1,0:T(8,128)} %get-tuple-element.41), channel_id=19, source_target_pairs={{0,1},{1,2},{2,3},{3,4},{4,5},{5,6},{6,7},{7,0},{8,9},{9,10},{10,1... | collective-permute-start | bytes 1376264 | tf_op jit(solution)/vmap(transpose(jvp()))/dot_general | solution.py:21
  473.3 64.9 %copy-start.11 = (f32[1,224,512]{2,1,0:T(8,128)S(1)}, f32[1,224,512]{2,1,0:T(8,128)}, u32[]{:S(2)}) copy-start(f32[1,224,512]{2,1,0:T(8,128)} %copy-done.10) | copy-start | bytes 1376260
  473.3 66.0 %copy-start.13 = (f32[1,224,512]{2,1,0:T(8,128)S(1)}, f32[1,224,512]{2,1,0:T(8,128)}, u32[]{:S(2)}) copy-start(f32[1,224,512]{2,1,0:T(8,128)} %copy-done.12) | copy-start | bytes 1376260
  473.4 14.1 %collective-permute-start.12 = (f32[1,64,1792]{2,1,0:T(8,128)S(1)}, f32[1,64,1792]{2,1,0:T(8,128)}, u32[]{:S(2)}, u32[]{:S(2)}) collective-permute-start(f32[1,64,1792]{2,1,0:T(8,128)S(1)} %broadcast_select_fusion.30), channel_id=22, source_target_pairs={{0,1},{1,2},{2,3},{3,4},{4,5},{5,6},{6,7},{7,0},{8,9},{9,10},{10,1... | collective-permute-start | bytes 1376264 | tf_op jit(solution)/vmap(transpose(jvp()))/dot_general | solution.py:21
  475.2 12.9 %collective-permute-start.13 = (f32[1,64,1792]{2,1,0:T(8,128)S(1)}, f32[1,64,1792]{2,1,0:T(8,128)S(1)}, u32[]{:S(2)}, u32[]{:S(2)}) collective-permute-start(f32[1,64,1792]{2,1,0:T(8,128)S(1)} %broadcast_select_fusion.31), channel_id=21, source_target_pairs={{0,7},{1,0},{2,1},{3,2},{4,3},{5,4},{6,5},{7,6},{8,15},{9,8},{10,9... | collective-permute-start | bytes 1376264 | tf_op jit(solution)/vmap(transpose(jvp()))/dot_general | solution.py:21
  490.0 13.9 %collective-permute-start.14 = (f32[1,64,1792]{2,1,0:T(8,128)}, f32[1,64,1792]{2,1,0:T(8,128)S(1)}, u32[]{:S(2)}, u32[]{:S(2)}) collective-permute-start(f32[1,64,1792]{2,1,0:T(8,128)} %get-tuple-element.482), channel_id=24, source_target_pairs={{0,1},{1,2},{2,3},{3,4},{4,5},{5,6},{6,7},{7,0},{8,9},{9,10},{10,1... | collective-permute-start | bytes 1376264 | tf_op jit(solution)/vmap(transpose(jvp()))/dot_general | solution.py:21
  491.7 12.2 %collective-permute-start.15 = (f32[1,64,1792]{2,1,0:T(8,128)S(1)}, f32[1,64,1792]{2,1,0:T(8,128)}, u32[]{:S(2)}, u32[]{:S(2)}) collective-permute-start(f32[1,64,1792]{2,1,0:T(8,128)S(1)} %get-tuple-element.483), channel_id=23, source_target_pairs={{0,7},{1,0},{2,1},{3,2},{4,3},{5,4},{6,5},{7,6},{8,15},{9,8},{10,9... | collective-permute-start | bytes 1376264 | tf_op jit(solution)/vmap(transpose(jvp()))/dot_general | solution.py:21
  506.9 13.6 %collective-permute-start.12 = (f32[1,64,1792]{2,1,0:T(8,128)S(1)}, f32[1,64,1792]{2,1,0:T(8,128)}, u32[]{:S(2)}, u32[]{:S(2)}) collective-permute-start(f32[1,64,1792]{2,1,0:T(8,128)S(1)} %broadcast_select_fusion.30), channel_id=22, source_target_pairs={{0,1},{1,2},{2,3},{3,4},{4,5},{5,6},{6,7},{7,0},{8,9},{9,10},{10,1... | collective-permute-start | bytes 1376264 | tf_op jit(solution)/vmap(transpose(jvp()))/dot_general | solution.py:21
  508.8 11.7 %collective-permute-start.13 = (f32[1,64,1792]{2,1,0:T(8,128)S(1)}, f32[1,64,1792]{2,1,0:T(8,128)S(1)}, u32[]{:S(2)}, u32[]{:S(2)}) collective-permute-start(f32[1,64,1792]{2,1,0:T(8,128)S(1)} %broadcast_select_fusion.31), channel_id=21, source_target_pairs={{0,7},{1,0},{2,1},{3,2},{4,3},{5,4},{6,5},{7,6},{8,15},{9,8},{10,9... | collective-permute-start | bytes 1376264 | tf_op jit(solution)/vmap(transpose(jvp()))/dot_general | solution.py:21
  522.4 10.8 %collective-permute-start.14 = (f32[1,64,1792]{2,1,0:T(8,128)}, f32[1,64,1792]{2,1,0:T(8,128)S(1)}, u32[]{:S(2)}, u32[]{:S(2)}) collective-permute-start(f32[1,64,1792]{2,1,0:T(8,128)} %get-tuple-element.482), channel_id=24, source_target_pairs={{0,1},{1,2},{2,3},{3,4},{4,5},{5,6},{6,7},{7,0},{8,9},{9,10},{10,1... | collective-permute-start | bytes 1376264 | tf_op jit(solution)/vmap(transpose(jvp()))/dot_general | solution.py:21
  523.5 9.7 %collective-permute-start.15 = (f32[1,64,1792]{2,1,0:T(8,128)S(1)}, f32[1,64,1792]{2,1,0:T(8,128)}, u32[]{:S(2)}, u32[]{:S(2)}) collective-permute-start(f32[1,64,1792]{2,1,0:T(8,128)S(1)} %get-tuple-element.483), channel_id=23, source_target_pairs={{0,7},{1,0},{2,1},{3,2},{4,3},{5,4},{6,5},{7,6},{8,15},{9,8},{10,9... | collective-permute-start | bytes 1376264 | tf_op jit(solution)/vmap(transpose(jvp()))/dot_general | solution.py:21
  535.1 95.2 %collective-permute-start.27 = (f32[1,64,1792]{2,1,0:T(8,128)}, f32[1,64,1792]{2,1,0:T(8,128)}, u32[]{:S(2)}, u32[]{:S(2)}) collective-permute-start(f32[1,64,1792]{2,1,0:T(8,128)} %get-tuple-element.43), channel_id=25, source_target_pairs={{0,1},{1,2},{2,3},{3,4},{4,5},{5,6},{6,7},{7,0},{8,9},{9,10},{10,1... | collective-permute-start | bytes 1376264 | tf_op jit(solution)/vmap(transpose(jvp()))/dot_general | solution.py:21
  543.9 186.1 %all-gather.12.cloned.1.call-start = ((), (), s32[]{:S(2)}) async-start(), calls=%async_computation.1 | async-start | bytes 4128768 | tf_op jit(solution)/reshape | solution.py:52
  544.0 85.2 %copy-start.15 = (f32[1,64,1792]{2,1,0:T(8,128)S(1)}, f32[1,64,1792]{2,1,0:T(8,128)}, u32[]{:S(2)}) copy-start(f32[1,64,1792]{2,1,0:T(8,128)} %copy-done.14) | copy-start | bytes 1376260
  544.2 15.9 %collective-permute-start = (f32[1,64,1792]{2,1,0:T(8,128)S(1)}, f32[1,64,1792]{2,1,0:T(8,128)}, u32[]{:S(2)}, u32[]{:S(2)}) collective-permute-start(f32[1,64,1792]{2,1,0:T(8,128)S(1)} %broadcast_select_fusion.24), channel_id=3, source_target_pairs={{0,1},{1,2},{2,3},{3,4},{4,5},{5,6},{6,7},{7,0},{8,9},{9,10},{10,1... | collective-permute-start | bytes 1376264 | tf_op jit(solution)/vmap(transpose(jvp()))/dot_general | solution.py:20
  545.8 16.9 %collective-permute-start.1 = (f32[1,64,1792]{2,1,0:T(8,128)S(1)}, f32[1,64,1792]{2,1,0:T(8,128)S(1)}, u32[]{:S(2)}, u32[]{:S(2)}) collective-permute-start(f32[1,64,1792]{2,1,0:T(8,128)S(1)} %broadcast_select_fusion.25), channel_id=2, source_target_pairs={{0,7},{1,0},{2,1},{3,2},{4,3},{5,4},{6,5},{7,6},{8,15},{9,8},{10,9... | collective-permute-start | bytes 1376264 | tf_op jit(solution)/vmap(transpose(jvp()))/dot_general | solution.py:20
  564.6 22.9 %collective-permute-start.2 = (f32[1,64,1792]{2,1,0:T(8,128)}, f32[1,64,1792]{2,1,0:T(8,128)S(1)}, u32[]{:S(2)}, u32[]{:S(2)}) collective-permute-start(f32[1,64,1792]{2,1,0:T(8,128)} %get-tuple-element.455), channel_id=5, source_target_pairs={{0,1},{1,2},{2,3},{3,4},{4,5},{5,6},{6,7},{7,0},{8,9},{9,10},{10,1... | collective-permute-start | bytes 1376264 | tf_op jit(solution)/vmap(transpose(jvp()))/dot_general | solution.py:20
  564.6 22.9 %collective-permute-start.3 = (f32[1,64,1792]{2,1,0:T(8,128)S(1)}, f32[1,64,1792]{2,1,0:T(8,128)}, u32[]{:S(2)}, u32[]{:S(2)}) collective-permute-start(f32[1,64,1792]{2,1,0:T(8,128)S(1)} %get-tuple-element.456), channel_id=4, source_target_pairs={{0,7},{1,0},{2,1},{3,2},{4,3},{5,4},{6,5},{7,6},{8,15},{9,8},{10,9... | collective-permute-start | bytes 1376264 | tf_op jit(solution)/vmap(transpose(jvp()))/dot_general | solution.py:20
  590.5 21.4 %collective-permute-start = (f32[1,64,1792]{2,1,0:T(8,128)S(1)}, f32[1,64,1792]{2,1,0:T(8,128)}, u32[]{:S(2)}, u32[]{:S(2)}) collective-permute-start(f32[1,64,1792]{2,1,0:T(8,128)S(1)} %broadcast_select_fusion.24), channel_id=3, source_target_pairs={{0,1},{1,2},{2,3},{3,4},{4,5},{5,6},{6,7},{7,0},{8,9},{9,10},{10,1... | collective-permute-start | bytes 1376264 | tf_op jit(solution)/vmap(transpose(jvp()))/dot_general | solution.py:20
  590.6 21.2 %collective-permute-start.1 = (f32[1,64,1792]{2,1,0:T(8,128)S(1)}, f32[1,64,1792]{2,1,0:T(8,128)S(1)}, u32[]{:S(2)}, u32[]{:S(2)}) collective-permute-start(f32[1,64,1792]{2,1,0:T(8,128)S(1)} %broadcast_select_fusion.25), channel_id=2, source_target_pairs={{0,7},{1,0},{2,1},{3,2},{4,3},{5,4},{6,5},{7,6},{8,15},{9,8},{10,9... | collective-permute-start | bytes 1376264 | tf_op jit(solution)/vmap(transpose(jvp()))/dot_general | solution.py:20
  613.7 12.1 %collective-permute-start.2 = (f32[1,64,1792]{2,1,0:T(8,128)}, f32[1,64,1792]{2,1,0:T(8,128)S(1)}, u32[]{:S(2)}, u32[]{:S(2)}) collective-permute-start(f32[1,64,1792]{2,1,0:T(8,128)} %get-tuple-element.455), channel_id=5, source_target_pairs={{0,1},{1,2},{2,3},{3,4},{4,5},{5,6},{6,7},{7,0},{8,9},{9,10},{10,1... | collective-permute-start | bytes 1376264 | tf_op jit(solution)/vmap(transpose(jvp()))/dot_general | solution.py:20
  613.7 12.1 %collective-permute-start.3 = (f32[1,64,1792]{2,1,0:T(8,128)S(1)}, f32[1,64,1792]{2,1,0:T(8,128)}, u32[]{:S(2)}, u32[]{:S(2)}) collective-permute-start(f32[1,64,1792]{2,1,0:T(8,128)S(1)} %get-tuple-element.456), channel_id=4, source_target_pairs={{0,7},{1,0},{2,1},{3,2},{4,3},{5,4},{6,5},{7,6},{8,15},{9,8},{10,9... | collective-permute-start | bytes 1376264 | tf_op jit(solution)/vmap(transpose(jvp()))/dot_general | solution.py:20
  627.7 89.1 %collective-permute-start.24 = (f32[1,64,1792]{2,1,0:T(8,128)}, f32[1,64,1792]{2,1,0:T(8,128)}, u32[]{:S(2)}, u32[]{:S(2)}) collective-permute-start(f32[1,64,1792]{2,1,0:T(8,128)} %get-tuple-element.37), channel_id=6, source_target_pairs={{0,1},{1,2},{2,3},{3,4},{4,5},{5,6},{6,7},{7,0},{8,9},{9,10},{10,1... | collective-permute-start | bytes 1376264 | tf_op jit(solution)/vmap(transpose(jvp()))/dot_general | solution.py:20
  634.9 139.9 %all-gather.10.cloned.1.call-start = ((), (), s32[]{:S(2)}) async-start(), calls=%async_computation | async-start | bytes 4128768 | tf_op jit(solution)/reshape | solution.py:52
  635.0 14.6 %collective-permute-start.4 = (f32[1,64,1792]{2,1,0:T(8,128)S(1)}, f32[1,64,1792]{2,1,0:T(8,128)S(1)}, u32[]{:S(2)}, u32[]{:S(2)}) collective-permute-start(f32[1,64,1792]{2,1,0:T(8,128)S(1)} %broadcast_select_fusion.26), channel_id=9, source_target_pairs={{0,1},{1,2},{2,3},{3,4},{4,5},{5,6},{6,7},{7,0},{8,9},{9,10},{10,1... | collective-permute-start | bytes 1376264 | tf_op jit(solution)/vmap(transpose(jvp()))/dot_general | solution.py:20
  635.6 18.8 %collective-permute-start.5 = (f32[1,64,1792]{2,1,0:T(8,128)S(1)}, f32[1,64,1792]{2,1,0:T(8,128)S(1)}, u32[]{:S(2)}, u32[]{:S(2)}) collective-permute-start(f32[1,64,1792]{2,1,0:T(8,128)S(1)} %broadcast_select_fusion.27), channel_id=8, source_target_pairs={{0,7},{1,0},{2,1},{3,2},{4,3},{5,4},{6,5},{7,6},{8,15},{9,8},{10,9... | collective-permute-start | bytes 1376264 | tf_op jit(solution)/vmap(transpose(jvp()))/dot_general | solution.py:20
  655.2 24.3 %collective-permute-start.6 = (f32[1,64,1792]{2,1,0:T(8,128)}, f32[1,64,1792]{2,1,0:T(8,128)S(1)}, u32[]{:S(2)}, u32[]{:S(2)}) collective-permute-start(f32[1,64,1792]{2,1,0:T(8,128)} %get-tuple-element.464), channel_id=11, source_target_pairs={{0,1},{1,2},{2,3},{3,4},{4,5},{5,6},{6,7},{7,0},{8,9},{9,10},{10,1... | collective-permute-start | bytes 1376264 | tf_op jit(solution)/vmap(transpose(jvp()))/dot_general | solution.py:20
  658.8 23.1 %collective-permute-start.7 = (f32[1,64,1792]{2,1,0:T(8,128)S(1)}, f32[1,64,1792]{2,1,0:T(8,128)}, u32[]{:S(2)}, u32[]{:S(2)}) collective-permute-start(f32[1,64,1792]{2,1,0:T(8,128)S(1)} %get-tuple-element.465), channel_id=10, source_target_pairs={{0,7},{1,0},{2,1},{3,2},{4,3},{5,4},{6,5},{7,6},{8,15},{9,8},{10,9... | collective-permute-start | bytes 1376264 | tf_op jit(solution)/vmap(transpose(jvp()))/dot_general | solution.py:20
  683.1 20.7 %collective-permute-start.4 = (f32[1,64,1792]{2,1,0:T(8,128)S(1)}, f32[1,64,1792]{2,1,0:T(8,128)S(1)}, u32[]{:S(2)}, u32[]{:S(2)}) collective-permute-start(f32[1,64,1792]{2,1,0:T(8,128)S(1)} %broadcast_select_fusion.26), channel_id=9, source_target_pairs={{0,1},{1,2},{2,3},{3,4},{4,5},{5,6},{6,7},{7,0},{8,9},{9,10},{10,1... | collective-permute-start | bytes 1376264 | tf_op jit(solution)/vmap(transpose(jvp()))/dot_general | solution.py:20
  683.3 20.4 %collective-permute-start.5 = (f32[1,64,1792]{2,1,0:T(8,128)S(1)}, f32[1,64,1792]{2,1,0:T(8,128)S(1)}, u32[]{:S(2)}, u32[]{:S(2)}) collective-permute-start(f32[1,64,1792]{2,1,0:T(8,128)S(1)} %broadcast_select_fusion.27), channel_id=8, source_target_pairs={{0,7},{1,0},{2,1},{3,2},{4,3},{5,4},{6,5},{7,6},{8,15},{9,8},{10,9... | collective-permute-start | bytes 1376264 | tf_op jit(solution)/vmap(transpose(jvp()))/dot_general | solution.py:20
  704.6 10.8 %collective-permute-start.6 = (f32[1,64,1792]{2,1,0:T(8,128)}, f32[1,64,1792]{2,1,0:T(8,128)S(1)}, u32[]{:S(2)}, u32[]{:S(2)}) collective-permute-start(f32[1,64,1792]{2,1,0:T(8,128)} %get-tuple-element.464), channel_id=11, source_target_pairs={{0,1},{1,2},{2,3},{3,4},{4,5},{5,6},{6,7},{7,0},{8,9},{9,10},{10,1... | collective-permute-start | bytes 1376264 | tf_op jit(solution)/vmap(transpose(jvp()))/dot_general | solution.py:20
  704.6 10.8 %collective-permute-start.7 = (f32[1,64,1792]{2,1,0:T(8,128)S(1)}, f32[1,64,1792]{2,1,0:T(8,128)}, u32[]{:S(2)}, u32[]{:S(2)}) collective-permute-start(f32[1,64,1792]{2,1,0:T(8,128)S(1)} %get-tuple-element.465), channel_id=10, source_target_pairs={{0,7},{1,0},{2,1},{3,2},{4,3},{5,4},{6,5},{7,6},{8,15},{9,8},{10,9... | collective-permute-start | bytes 1376264 | tf_op jit(solution)/vmap(transpose(jvp()))/dot_general | solution.py:20
  716.6 9.8 %collective-permute-start.25 = (f32[1,64,1792]{2,1,0:T(8,128)S(1)}, f32[1,64,1792]{2,1,0:T(8,128)S(1)}, u32[]{:S(2)}, u32[]{:S(2)}) collective-permute-start(f32[1,64,1792]{2,1,0:T(8,128)S(1)} %get-tuple-element.39), channel_id=12, source_target_pairs={{0,1},{1,2},{2,3},{3,4},{4,5},{5,6},{6,7},{7,0},{8,9},{9,10},{10,1... | collective-permute-start | bytes 1376264 | tf_op jit(solution)/vmap(transpose(jvp()))/dot_general | solution.py:20
  (24 other events, 198.0 us)
Sparse Core Ops, SparseCore 0:
  544.0 67.2 all-gather.13
  635.0 65.7 all-gather.11
  730.1 44.6 all-gather.9
where the time goes:
time: 801 us; the launch traced here: 790 us
  matrix products  339 us (42%)
  waiting for transfers between devices  149 us (19%)
  starting transfers between devices  92.7 us (12%)
  other arithmetic  86 us (11%)
  local copies, waits for them, and re-layouts  83.8 us (10%)
  loops' own time  24.7 us (3%)
  between operations  14.9 us (2%)
    dot_general x11, matrix products, layer(): gate = jnp.dot(a, w['w_gate'], preferred_element_type=jnp.float32)  128 us
    dot_general x11, matrix products, layer(): up = jnp.dot(a, w['w_up'], preferred_element_type=jnp.float32)  118 us
    dot_general x11, matrix products, matmul(): jnp.dot(a, w, preferred_element_type=jnp.float32).astype(jnp.bfloat16)  92.5 us
    unnamed x55, local copies, waits for them, and re-layouts  76.1 us
    dot_general x18, waiting for transfers between devices, layer(): gate = jnp.dot(a, w['w_gate'], preferred_element_type=jnp.float32)  62.4 us
    reshape x3, waiting for transfers between devices, step(): t.reshape(-1, *t.shape[2:])  44.8 us
    dot_general x18, starting transfers between devices, matmul(): jnp.dot(a, w, preferred_element_type=jnp.float32).astype(jnp.bfloat16)  34.6 us
    dot_general x18, starting transfers between devices, layer(): gate = jnp.dot(a, w['w_gate'], preferred_element_type=jnp.float32)  29.2 us
  transfers between devices with their start and end apart: 57, of which 27 were waited for; matrix products, arithmetic and copies ran while one was open for 38% of the time, Pallas kernels for 0%

commit v1 on v0

v1 whole, which is shorter than its diff:
```python
import functools

import jax
import jax.numpy as jnp
from jax import lax
from jax.experimental import pallas as pl
from jax.experimental.pallas import tpu as pltpu
from jax.sharding import PartitionSpec as P

BF = jnp.bfloat16
F32 = jnp.float32
TILE = 512
TOK = 1024
COLS = 256
VMEM_LIMIT = 67043328


def mm(a, b):
    return jnp.dot(a, b, preferred_element_type=F32)


def mm_nt(a, b):
    return lax.dot_general(a, b, (((1,), (1,)), ((), ())), preferred_element_type=F32)


def normed(h):
    wide = h.astype(F32)
    scale = lax.rsqrt(jnp.mean(wide * wide, -1, keepdims=True) + 1e-6)
    return (wide * scale).astype(BF)


def forward_kernel(x_ref, dy_ref, wg_ref, wu_ref, wd_ref, a1_ref, a1t_ref, a2_ref, a2t_ref, h_ref, dyt_ref):
    x = x_ref[0]
    a = normed(x)
    a1_ref[...] = a
    a1t_ref[...] = a.T
    dyt_ref[...] = dy_ref[0].T
    total = None
    for j in range(wg_ref.shape[2] // COLS):
        cols = slice(j * COLS, (j + 1) * COLS)
        gate = mm(a, wg_ref[0, :, cols])
        up = mm(a, wu_ref[0, :, cols])
        act = (gate * jax.nn.sigmoid(gate) * up).astype(BF)
        part = mm(act, wd_ref[0, cols, :])
        total = part if total is None else total + part
    h = (x.astype(F32) + total.astype(BF).astype(F32)).astype(BF)
    h_ref[...] = h
    a2 = normed(h)
    a2_ref[...] = a2
    a2t_ref[...] = a2.T


def forward(x, dy, wg, wu, wd):
    _, tokens, d = x.shape
    ff = wg.shape[2]
    row = pl.BlockSpec((1, TILE, d), lambda i: (0, i, 0))
    out = pl.BlockSpec((TILE, d), lambda i: (i, 0))
    out_t = pl.BlockSpec((d, TILE), lambda i: (0, i))
    w_in = pl.BlockSpec((1, d, ff), lambda i: (0, 0, 0))
    w_out = pl.BlockSpec((1, ff, d), lambda i: (0, 0, 0))
    straight, turned = jax.ShapeDtypeStruct((tokens, d), BF), jax.ShapeDtypeStruct((d, tokens), BF)
    return pl.pallas_call(
        forward_kernel,
        grid=(tokens // TILE,),
        in_specs=[row, row, w_in, w_in, w_out],
        out_specs=[out, out_t, out, out_t, out, out_t],
        out_shape=[straight, turned, straight, turned, straight, turned],
        compiler_params=pltpu.CompilerParams(vmem_limit_bytes=VMEM_LIMIT, dimension_semantics=("arbitrary",)),
        name="forward",
    )(x, dy, wg, wu, wd)


def tile_grads(top, layer, j, t, refs):
    A, AT, D, DT, DA, WG, WU, WD, GU, DWT = refs
    rows = slice(t * TOK, (t + 1) * TOK)
    cols = pl.ds(pl.multiple_of(j * COLS, COLS), COLS)
    wg, wu = WG[layer, :, cols], WU[layer, :, cols]
    a, dy = A[rows, :], D[rows, :]
    gate, up = mm(a, wg), mm(a, wu)
    dact = mm_nt(dy, WD[layer, cols, :]).astype(BF).astype(F32)
    sig = jax.nn.sigmoid(gate)
    silu = gate * sig
    act = (silu * up).astype(BF)
    dup = (dact * silu).astype(BF)
    dgate = (dact * up * (sig + silu * (1.0 - sig))).astype(BF)
    at, dt = AT[:, rows], DT[:, rows]
    n, rows_of, _ = GU.shape
    half = rows_of // 2
    dwt = mm(dt, act)
    dwg = mm(at, dgate).reshape(n, half, COLS)
    dwu = mm(at, dup).reshape(n, half, COLS)
    if t == 0:
        DWT[...] = dwt
        GU[:, :half, :] = dwg
        GU[:, half:, :] = dwu
    else:
        DWT[...] += dwt
        GU[:, :half, :] += dwg
        GU[:, half:, :] += dwu
    if top:
        da = mm_nt(dgate, wg) + mm_nt(dup, wu)

        @pl.when(j == 0)
        def _():
            DA[rows, :] = da

        @pl.when(j > 0)
        def _():
            DA[rows, :] += da


def through_norm(t, A_, D, DT, H, DA):
    rows = slice(t * TILE, (t + 1) * TILE)
    h = H[rows, :].astype(F32)
    s = lax.rsqrt(jnp.mean(h * h, -1, keepdims=True) + 1e-6)
    da = DA[rows, :].astype(BF).astype(F32)
    dh = da * s - h * (s * s * s * jnp.mean(da * h, -1, keepdims=True))
    dh = (D[rows, :].astype(F32) + dh.astype(BF).astype(F32)).astype(BF)
    D[rows, :] = dh
    DT[:, rows] = dh.T


def grads_kernel(
    n, dy_h, a1_h, a1t_h, a2_h, a2t_h, h_h, dyt_h, wg_h, wu_h, wd_h,
    gu_o, gd_o,
    A, AT, D, DT, H, DA, WG, WU, WD, GU, GUB, DWT, DW, DWB, load, wsem, hsem, osem,
):
    tokens, d = A.shape
    nt = tokens // TOK
    ff = WG.shape[2]
    nj = ff // COLS

    def tile_loads(t, a_h, at_h, with_dy):
        rows = slice(t * TOK, (t + 1) * TOK)
        pairs = [(a_h.at[rows, :], A.at[rows, :]), (at_h.at[:, rows], AT.at[:, rows])]
        if with_dy:
            pairs += [(dy_h.at[0, rows, :], D.at[rows, :]), (dyt_h.at[:, rows], DT.at[:, rows])]
        return [pltpu.make_async_copy(s, o, load.at[t, i]) for i, (s, o) in enumerate(pairs)]

    weights = [
        pltpu.make_async_copy(s.at[l], o.at[l], wsem.at[l, i])
        for l in (1, 0) for i, (s, o) in enumerate(((wg_h, WG), (wu_h, WU), (wd_h, WD)))
    ]
    for c in weights[:3]:
        c.start()
    for t in range(nt):
        for c in tile_loads(t, a2_h, a2t_h, True):
            c.start()
    hcopy = pltpu.make_async_copy(h_h, H, hsem)
    hcopy.start()
    for c in weights[3:]:
        c.start()
    for c in weights[:3]:
        c.wait()

    refs = (A, AT, D, DT, DA, WG, WU, WD, GU, DWT)

    def finish(layer, j):
        @pl.when((j > 0) if layer else (j >= 0))
        def _():
            pltpu.make_async_copy(GUB, gu_o.at[0, :, 0], osem.at[0]).wait()
        GUB[...] = GU[...].astype(BF)
        pltpu.make_async_copy(GUB, gu_o.at[layer, :, j], osem.at[0]).start()
        DW[pl.ds(pl.multiple_of(j * COLS, COLS), COLS), :] = DWT[...].T

    def top_block(j, carry):
        for t in range(nt):
            @pl.when(j == 0)
            def _():
                for c in tile_loads(t, a2_h, a2t_h, True):
                    c.wait()
            tile_grads(True, 1, j, t, refs)

            @pl.when(j == nj - 1)
            def _():
                for c in tile_loads(t, a1_h, a1t_h, False):
                    c.start()
        finish(1, j)
        return carry

    lax.fori_loop(0, nj, top_block, 0)
    DWB[...] = DW[...].astype(BF)
    pltpu.make_async_copy(DWB, gd_o.at[1], osem.at[1]).start()
    hcopy.wait()
    for c in weights[3:]:
        c.wait()
    for t in range(tokens // TILE):
        through_norm(t, A, D, DT, H, DA)

    def low_block(j, carry):
        for t in range(nt):
            @pl.when(j == 0)
            def _():
                for c in tile_loads(t, a1_h, a1t_h, False):
                    c.wait()
            tile_grads(False, 0, j, t, refs)
        finish(0, j)
        return carry

    lax.fori_loop(0, nj, low_block, 0)
    pltpu.make_async_copy(DWB, gd_o.at[1], osem.at[1]).wait()
    DWB[...] = DW[...].astype(BF)
    pltpu.make_async_copy(DWB, gd_o.at[0], osem.at[1]).start()
    pltpu.make_async_copy(GUB, gu_o.at[0, :, 0], osem.at[0]).wait()
    pltpu.make_async_copy(DWB, gd_o.at[0], osem.at[1]).wait()


def grads(n, dy, a1, a1t, a2, a2t, h, dyt, wg, wu, wd):
    tokens, d = a1.shape
    layers, _, ff = wg.shape
    nj, nt = ff // COLS, tokens // TOK
    block = (n, 2 * d // n, COLS)
    any_ = pl.BlockSpec(memory_space=pl.ANY)
    return pl.pallas_call(
        functools.partial(grads_kernel, n),
        in_specs=[any_] * 10,
        out_specs=[any_] * 2,
        out_shape=[jax.ShapeDtypeStruct((layers, n, nj, *block[1:]), BF), jax.ShapeDtypeStruct((layers, ff, d), BF)],
        scratch_shapes=[
            pltpu.VMEM((tokens, d), BF), pltpu.VMEM((d, tokens), BF), pltpu.VMEM((tokens, d), BF), pltpu.VMEM((d, tokens), BF),
            pltpu.VMEM((tokens, d), BF), pltpu.VMEM((tokens, d), F32),
            pltpu.VMEM((layers, d, ff), BF), pltpu.VMEM((layers, d, ff), BF), pltpu.VMEM((layers, ff, d), BF),
            pltpu.VMEM(block, F32), pltpu.VMEM(block, BF), pltpu.VMEM((d, COLS), F32), pltpu.VMEM((ff, d), F32), pltpu.VMEM((ff, d), BF),
            pltpu.SemaphoreType.DMA((nt, 4)), pltpu.SemaphoreType.DMA((2, 3)), pltpu.SemaphoreType.DMA, pltpu.SemaphoreType.DMA((2,)),
        ],
        compiler_params=pltpu.CompilerParams(vmem_limit_bytes=VMEM_LIMIT),
        name="grads",
    )(dy, a1, a1t, a2, a2t, h, dyt, wg, wu, wd)


def adamw(w, m, v, g):
    m = 0.9 * m + 0.1 * g
    v = 0.95 * v + 0.05 * g * g
    step = m * lax.rsqrt(v + 1e-8) + 0.1 * w
    return (w - 0.02 * step).astype(BF), m, v


def solution(mesh):
    n = mesh.shape["dp"]

    def step(x, dy, wg, wu, wd, mg, mu, md, vg, vu, vd):
        layers, d, ff = wg.shape
        nj, half = ff // COLS, d // n
        a1, a1t, a2, a2t, h, dyt = forward(x, dy, wg, wu, wd)
        gu, gd = grads(n, dy, a1, a1t, a2, a2t, h, dyt, wg, wu, wd)
        out = []
        me = lax.axis_index("dp")
        new = {}
        for l in range(layers - 1, -1, -1):
            gul = lax.psum_scatter(gu[l], "dp", scatter_dimension=0, tiled=True)
            gul = gul.reshape(nj, 2, half, COLS).transpose(1, 2, 0, 3).reshape(2, half, ff).astype(F32)
            gdl = lax.psum_scatter(gd[l], "dp", scatter_dimension=0, tiled=True).astype(F32)
            for k, (w, m, v, g) in enumerate(((wg, mg, vg, gul[0]), (wu, mu, vu, gul[1]), (wd, md, vd, gdl))):
                mine = lax.dynamic_slice_in_dim(w[l], me * g.shape[0], g.shape[0], 0).astype(F32)
                nw, nm, nv = adamw(mine, m[l], v[l], g)
                new[l, k] = (lax.all_gather(nw, "dp", axis=0, tiled=True), nm, nv)
        return tuple(jnp.stack([new[l, k][which] for l in range(layers)]) for which in range(3) for k in range(3))

    data, whole, own = P(("rep", "dp"), None, None), P(), P(None, "dp", None)
    return jax.shard_map(
        step, mesh=mesh, in_specs=(data,) * 2 + (whole,) * 3 + (own,) * 6,
        out_specs=(P("rep", None, None),) * 3 + (P("rep", "dp", None),) * 6, check_vma=False,
    )
```

time: 801 us -> 599 us (0.75); the launches traced: 790 us -> 598 us
  matrix products: 339 us -> 0 us
  waiting for transfers between devices: 149 us -> 358 us
  Pallas kernels: 0 us -> 173 us
  starting transfers between devices: 92.7 us -> 0.85 us
  other arithmetic: 86 us -> 26.4 us
  local copies, waits for them, and re-layouts: 83.8 us -> 26.5 us
  loops' own time: 24.7 us -> 0 us
    dot_general x33 -> x0, matrix products: 339 us -> none  [the longest x11 128 us: layer(): gate = jnp.dot(a, w['w_gate'], preferred_element_type=jnp.float32)]
    all_gather x0 -> x6, waiting for transfers between devices: none -> 196 us  [step(): new[l, k] = (lax.all_gather(nw, 'dp', axis=0, tiled=True), nm, nv)]
    pallas_call x0 -> x2, Pallas kernels: none -> 173 us  [the longest x1 141 us: grads(): pl.pallas_call(functools.partial(grads_kernel, n), in_specs=[any_] * 10,...]
    reduce_scatter x0 -> x4, waiting for transfers between devices: none -> 158 us  [the longest x2 88.9 us: step(): gul = lax.psum_scatter(gu[l], 'dp', scatter_dimension=0, tiled=True)]
    dot_general x54 -> x0, waiting for transfers between devices: 104 us -> none  [the longest x18 62.4 us: layer(): gate = jnp.dot(a, w['w_gate'], preferred_element_type=jnp.float32)]
    dot_general x54 -> x0, starting transfers between devices: 92.5 us -> none  [the longest x18 34.6 us: matmul(): jnp.dot(a, w, preferred_element_type=jnp.float32).astype(jnp.bfloat16)]
    unnamed x55 -> x18, local copies, waits for them, and re-layouts: 76.1 us -> 0.61 us
    reshape x3 -> x0, waiting for transfers between devices: 44.8 us -> none  [step(): t.reshape(-1, *t.shape[2:])]
  transfers between devices with their start and end apart: 57 -> 10, of which waited for: 27 -> 10; matrix products, arithmetic and copies ran while one was open for 38% -> 7% of each run, Pallas kernels for 0% -> 0%
where the time goes in v1:
time: 599 us; the launch traced here: 598 us
  waiting for transfers between devices  358 us (60%)
  Pallas kernels  173 us (29%)
  local copies, waits for them, and re-layouts  26.5 us (4%)
  other arithmetic  26.4 us (4%)
  between operations  14.4 us (2%)
    all_gather x6, waiting for transfers between devices, step(): new[l, k] = (lax.all_gather(nw, 'dp', axis=0, tiled=True), nm, nv)  196 us
    pallas_call x1, Pallas kernels, grads(): pl.pallas_call(functools.partial(grads_kernel, n), in_specs=[any_] * 10,...  141 us
    reduce_scatter x2, waiting for transfers between devices, step(): gul = lax.psum_scatter(gu[l], 'dp', scatter_dimension=0, tiled=True)  88.9 us
    reduce_scatter x2, waiting for transfers between devices, step(): lax.psum_scatter(gd[l], 'dp', scatter_dimension=0, tiled=True).astype(F32)  69.1 us
    pallas_call x1, Pallas kernels, forward(): pl.pallas_call(forward_kernel, grid=(tokens // TILE,), in_specs=[row, row...  32 us
    another operation x6, other arithmetic, step(): jnp.stack([new[l, k][which] for l in range(layers)])  18.1 us
  transfers between devices with their start and end apart: 10, of which 10 were waited for; matrix products, arithmetic and copies ran while one was open for 7% of the time, Pallas kernels for 0%

profile of v1, /device:TPU:22, one launch (start us, length us, event | category | flops | bytes accessed | tf_op | source)
XLA Modules:
  0.0 598.3 jit_solution(15989217446703029857)
XLA Ops:
  7.2 0.1 reduce-scatter.11.cloned.1.call-start
  7.3 32.0 %forward.1 = (bf16[4096,512]{1,0:T(8,128)(2,1)}, bf16[512,4096]{1,0:T(8,128)(2,1)}, bf16[4096,512]{1,0:T(8,128)(2,1)}, bf16[512,4096]{1,0:T(8,128)(2,1)}, bf16[4...) custom-call(bf16[1,4096,512]{2,1,0:T(8,128)(2,1)} %x_ref.1, bf16[1,4096,512]{2,1,0:T(8,128)(2,1)} %dy_h.1, ...), custom_call_target="tpu_custom_call" | custom-call | tf_op jit(solution)/shard_map/forward/pallas_call | solution.py:62
  39.3 140.7 %grads.1 = (bf16[2,8,7,128,256]{4,3,2,1,0:T(8,128)(2,1)}, bf16[2,1792,512]{2,1,0:T(8,128)(2,1)}) custom-call(bf16[1,4096,512]{2,1,0:T(8,128)(2,1)} %dy_h.1, bf16[4096,512]{1,0:T(8,128)(2,1)} %get-tuple-element.17.a1_h, bf16[512,4096]{1,0:T(8,128)(2,1)} %get-tuple-element.18.a1t_h, bf16[4096,512]{1,0:T(8,128)(2,1)} %get-tuple-element.19.a2_h, ...), custom_call_target="tpu_custom_call" | custom-call | tf_op jit(solution)/shard_map/grads/pallas_call | solution.py:214
  179.9 4.2 slice_bitcast_fusion.3
  184.1 0.1 reduce-scatter.11.cloned.1.call-update
  184.2 0.1 reduce-scatter.9.cloned.1.call-start
  184.3 0.7 reduce-scatter.9.cloned.1.call-update
  185.0 0.3 reduce-scatter.5.cloned.1.call-start
  185.3 7.2 %slice_bitcast_fusion.1 = (bf16[8,7,128,256]{3,2,1,0:T(8,128)(2,1)}, bf16[8,7,128,256]{3,2,1,0:T(8,128)(2,1)}) fusion(bf16[2,8,7,128,256]{4,3,2,1,0:T(8,128)(2,1)} %get-tuple-element.23), kind=kLoop, calls=%fused_computation.4 | loop fusion | bytes 14680064 | tf_op jit(solution)/shard_map/squeeze | solution.py:250
  192.5 0.1 reduce-scatter.5.cloned.1.call-update
  192.5 0.1 reduce-scatter.7.cloned.1.call-start
  192.6 0.6 reduce-scatter.7.cloned.1.call-update
  193.2 0.1 all-gather.15.cloned.1.call-start
  193.2 0.0 copy-start.6
  193.3 3.6 fusion.46
  196.9 29.3 %reduce-scatter.11.cloned.1.call-done = bf16[224,512]{1,0:T(8,128)(2,1)} async-done(((bf16[1792,512]{1,0:T(8,128)(2,1)}), bf16[224,512]{1,0:T(8,128)(2,1)}) %reduce-scatter.11.cloned.1.call-update) | async-done | bytes 229392 | tf_op jit(solution)/shard_map/reduce_scatter | solution.py:252
  226.2 39.8 %reduce-scatter.9.cloned.1.call-done = bf16[224,512]{1,0:T(8,128)(2,1)} async-done(((bf16[1792,512]{1,0:T(8,128)(2,1)}), bf16[224,512]{1,0:T(8,128)(2,1)}) %reduce-scatter.9.cloned.1.call-update) | async-done | bytes 229392 | tf_op jit(solution)/shard_map/reduce_scatter | solution.py:252
  266.0 2.9 fusion.16
  268.8 0.1 all-gather.15.cloned.1.call-update
  268.9 0.1 all-gather.17.cloned.1.call-start
  269.0 0.6 all-gather.17.cloned.1.call-update
  269.5 0.1 all-gather.11.cloned.1.call-start
  269.6 4.2 fusion.47
  273.8 41.0 %reduce-scatter.5.cloned.1.call-done = bf16[1,7,128,256]{3,2,1,0:T(8,128)(2,1)} async-done(((bf16[8,7,128,256]{3,2,1,0:T(8,128)(2,1)}), bf16[1,7,128,256]{3,2,1,0:T(8,128)(2,1)}) %reduce-scatter.5.cloned.1.call-update) | async-done | bytes 458768 | tf_op jit(solution)/shard_map/reduce_scatter | solution.py:250
  314.8 1.3 copy.37
  316.1 47.9 %reduce-scatter.7.cloned.1.call-done = bf16[1,7,128,256]{3,2,1,0:T(8,128)(2,1)} async-done(((bf16[8,7,128,256]{3,2,1,0:T(8,128)(2,1)}), bf16[1,7,128,256]{3,2,1,0:T(8,128)(2,1)}) %reduce-scatter.7.cloned.1.call-update) | async-done | bytes 458768 | tf_op jit(solution)/shard_map/reduce_scatter | solution.py:250
  364.0 1.4 copy.36
  365.4 0.1 fusion.49
  365.5 0.1 copy.32
  365.7 0.1 fusion.50
  365.7 0.1 copy.33
  365.9 2.3 fusion.10
  368.2 0.1 all-gather.11.cloned.1.call-update
  368.3 0.1 all-gather.13.cloned.1.call-start
  368.3 0.7 all-gather.13.cloned.1.call-update
  369.1 0.1 all-gather.9.cloned.1.call-start
  369.1 0.0 copy-start.2
  369.2 0.0 copy-start.4
  369.2 2.4 fusion.48
  371.6 0.1 copy.30
  371.7 0.1 copy.31
  371.9 1.2 fusion.4
  373.2 0.1 all-gather.9.cloned.1.call-update
  373.2 0.1 all-gather.7.cloned.1.call-start
  373.3 0.6 all-gather.7.cloned.1.call-update
  373.9 2.7 pad_maximum_fusion.5
  376.5 25.5 %all-gather.15.cloned.1.call-done = bf16[1792,512]{1,0:T(8,128)(2,1)} async-done(((bf16[224,512]{1,0:T(8,128)(2,1)}), bf16[1792,512]{1,0:T(8,128)(2,1)}) %all-gather.15.cloned.1.call-update) | async-done | bytes 1835024 | tf_op jit(solution)/shard_map/all_gather | solution.py:256
  402.0 36.7 %all-gather.17.cloned.1.call-done = bf16[1792,512]{1,0:T(8,128)(2,1)} async-done(((bf16[224,512]{1,0:T(8,128)(2,1)}), bf16[1792,512]{1,0:T(8,128)(2,1)}) %all-gather.17.cloned.1.call-update) | async-done | bytes 1835024 | tf_op jit(solution)/shard_map/all_gather | solution.py:256
  438.7 4.2 pad_maximum_fusion.2
  443.0 0.2 slice.118
  443.1 0.9 slice.119
  444.1 0.2 slice.116
  444.2 0.2 slice.117
  444.4 0.0 copy-start.3
  444.4 1.7 multiply_add_fusion.1
  446.1 1.4 pad_maximum_fusion.4
  447.5 0.3 multiply_add_fusion.3
  447.8 1.4 pad_maximum_fusion.3
  449.1 27.1 %all-gather.11.cloned.1.call-done = bf16[512,1792]{1,0:T(8,128)(2,1)} async-done(((bf16[64,1792]{1,0:T(8,128)(2,1)}), bf16[512,1792]{1,0:T(8,128)(2,1)}) %all-gather.11.cloned.1.call-update) | async-done | bytes 1835024 | tf_op jit(solution)/shard_map/all_gather | solution.py:256
  476.2 36.9 %all-gather.13.cloned.1.call-done = bf16[512,1792]{1,0:T(8,128)(2,1)} async-done(((bf16[64,1792]{1,0:T(8,128)(2,1)}), bf16[512,1792]{1,0:T(8,128)(2,1)}) %all-gather.13.cloned.1.call-update) | async-done | bytes 1835024 | tf_op jit(solution)/shard_map/all_gather | solution.py:256
  513.1 4.2 pad_maximum_fusion.1
  517.3 32.7 %all-gather.9.cloned.1.call-done = bf16[512,1792]{1,0:T(8,128)(2,1)} async-done(((bf16[64,1792]{1,0:T(8,128)(2,1)}), bf16[512,1792]{1,0:T(8,128)(2,1)}) %all-gather.9.cloned.1.call-update) | async-done | bytes 1835024 | tf_op jit(solution)/shard_map/all_gather | solution.py:256
  549.9 37.3 %all-gather.7.cloned.1.call-done = bf16[512,1792]{1,0:T(8,128)(2,1)} async-done(((bf16[64,1792]{1,0:T(8,128)(2,1)}), bf16[512,1792]{1,0:T(8,128)(2,1)}) %all-gather.7.cloned.1.call-update) | async-done | bytes 1835024 | tf_op jit(solution)/shard_map/all_gather | solution.py:256
  587.3 4.2 pad_maximum_fusion
  (10 shorter events, 0.0 us)
Async XLA Ops:
  7.2 219.0 %reduce-scatter.11.cloned.1.call-start = ((), (), s32[]{:S(2)}) async-start(), calls=%async_computation.12 | async-start | bytes 2064384 | tf_op jit(solution)/shard_map/reduce_scatter | solution.py:252
  184.2 81.8 %reduce-scatter.9.cloned.1.call-start = ((), (), s32[]{:S(2)}) async-start(), calls=%async_computation.10 | async-start | bytes 2064384 | tf_op jit(solution)/shard_map/reduce_scatter | solution.py:252
  185.0 129.8 %reduce-scatter.5.cloned.1.call-start = ((), (), s32[]{:S(2)}) async-start(), calls=%async_computation.4 | async-start | bytes 4128768 | tf_op jit(solution)/shard_map/reduce_scatter | solution.py:250
  192.5 171.5 %reduce-scatter.7.cloned.1.call-start = ((), (), s32[]{:S(2)}) async-start(), calls=%async_computation.6 | async-start | bytes 4128768 | tf_op jit(solution)/shard_map/reduce_scatter | solution.py:250
  193.2 208.9 %all-gather.15.cloned.1.call-start = ((), (), s32[]{:S(2)}) async-start(), calls=%async_computation.11 | async-start | bytes 2064384 | tf_op jit(solution)/shard_map/all_gather | solution.py:256
  193.2 72.7 %copy-start.6 = (f32[2,224,512]{2,1,0:T(8,128)S(1)}, f32[2,224,512]{2,1,0:T(8,128)}, u32[]{:S(2)}) copy-start(f32[2,224,512]{2,1,0:T(8,128)} %param.18) | copy-start | bytes 2752516
  268.9 169.8 %all-gather.17.cloned.1.call-start = ((), (), s32[]{:S(2)}) async-start(), calls=%async_computation.13 | async-start | bytes 2064384 | tf_op jit(solution)/shard_map/all_gather | solution.py:256
  269.5 206.6 %all-gather.11.cloned.1.call-start = ((), (), s32[]{:S(2)}) async-start(), calls=%async_computation.8 | async-start | bytes 2064384 | tf_op jit(solution)/shard_map/all_gather | solution.py:256
  364.0 1.9 copy-start
  364.0 1.9 copy-start.1
  368.3 144.8 %all-gather.13.cloned.1.call-start = ((), (), s32[]{:S(2)}) async-start(), calls=%async_computation.9 | async-start | bytes 2064384 | tf_op jit(solution)/shard_map/all_gather | solution.py:256
  369.1 180.9 %all-gather.9.cloned.1.call-start = ((), (), s32[]{:S(2)}) async-start(), calls=%async_computation.7 | async-start | bytes 2064384 | tf_op jit(solution)/shard_map/all_gather | solution.py:256
  369.1 2.8 copy-start.2
  369.2 2.7 copy-start.4
  373.2 214.0 %all-gather.7.cloned.1.call-start = ((), (), s32[]{:S(2)}) async-start(), calls=%async_computation.5 | async-start | bytes 2064384 | tf_op jit(solution)/shard_map/all_gather | solution.py:256
  444.4 3.1 copy-start.3
  444.4 3.1 copy-start.5
Sparse Core Ops, SparseCore 0:
  184.3 41.8 reduce-scatter.10
  229.2 36.7 reduce-scatter.8
  268.9 45.8 reduce-scatter.4
  317.6 46.3 reduce-scatter.6
  366.0 35.9 all-gather.14
  403.5 35.2 all-gather.16
  440.9 35.2 all-gather.10
  477.8 35.2 all-gather.12
  514.7 35.2 all-gather.8
  551.9 35.2 all-gather.6

commit v2 on v1

v2 whole, which is shorter than its diff:
```python
import functools

import jax
import jax.numpy as jnp
from jax import lax
from jax.experimental import pallas as pl
from jax.experimental.pallas import tpu as pltpu
from jax.sharding import PartitionSpec as P

BF = jnp.bfloat16
F32 = jnp.float32
TILE = 512
TOK = 1024
COLS = 256
WIDE = 256
SLOTS = 3
MESH = pl.DeviceIdType.MESH
VMEM_LIMIT = 67043328


def mm(a, b):
    return jnp.dot(a, b, preferred_element_type=F32)


def mm_nt(a, b):
    return lax.dot_general(a, b, (((1,), (1,)), ((), ())), preferred_element_type=F32)


def normed(h):
    wide = h.astype(F32)
    scale = lax.rsqrt(jnp.mean(wide * wide, -1, keepdims=True) + 1e-6)
    return (wide * scale).astype(BF)


def forward_kernel(x_ref, dy_ref, wg_ref, wu_ref, wd_ref, a1_ref, a1t_ref, a2_ref, a2t_ref, h_ref, dyt_ref):
    x = x_ref[0]
    a = normed(x)
    a1_ref[...] = a
    a1t_ref[...] = a.T
    dyt_ref[...] = dy_ref[0].T
    total = None
    for j in range(wg_ref.shape[2] // COLS):
        cols = slice(j * COLS, (j + 1) * COLS)
        gate = mm(a, wg_ref[0, :, cols])
        up = mm(a, wu_ref[0, :, cols])
        act = (gate * jax.nn.sigmoid(gate) * up).astype(BF)
        part = mm(act, wd_ref[0, cols, :])
        total = part if total is None else total + part
    h = (x.astype(F32) + total.astype(BF).astype(F32)).astype(BF)
    h_ref[...] = h
    a2 = normed(h)
    a2_ref[...] = a2
    a2t_ref[...] = a2.T


def forward(x, dy, wg, wu, wd):
    _, tokens, d = x.shape
    ff = wg.shape[2]
    row = pl.BlockSpec((1, TILE, d), lambda i: (0, i, 0))
    out = pl.BlockSpec((TILE, d), lambda i: (i, 0))
    out_t = pl.BlockSpec((d, TILE), lambda i: (0, i))
    w_in = pl.BlockSpec((1, d, ff), lambda i: (0, 0, 0))
    w_out = pl.BlockSpec((1, ff, d), lambda i: (0, 0, 0))
    straight, turned = jax.ShapeDtypeStruct((tokens, d), BF), jax.ShapeDtypeStruct((d, tokens), BF)
    return pl.pallas_call(
        forward_kernel,
        grid=(tokens // TILE,),
        in_specs=[row, row, w_in, w_in, w_out],
        out_specs=[out, out_t, out, out_t, out, out_t],
        out_shape=[straight, turned, straight, turned, straight, turned],
        compiler_params=pltpu.CompilerParams(vmem_limit_bytes=VMEM_LIMIT, dimension_semantics=("arbitrary",)),
        name="forward",
    )(x, dy, wg, wu, wd)


def tile_grads(top, layer, j, t, slot, refs):
    A, AT, D, DT, S, WG, WU, WD, GU, DWT = refs
    rows = slice(t * TOK, (t + 1) * TOK)
    cols = pl.ds(pl.multiple_of(j * COLS, COLS), COLS)
    wg, wu = WG[layer, :, cols], WU[layer, :, cols]
    a, dy = A[rows, :], D[rows, :]
    gate, up = mm(a, wg), mm(a, wu)
    dact = mm_nt(dy, WD[layer, cols, :]).astype(BF).astype(F32)
    sig = jax.nn.sigmoid(gate)
    silu = gate * sig
    act = (silu * up).astype(BF)
    dup = (dact * silu).astype(BF)
    dgate = (dact * up * (sig + silu * (1.0 - sig))).astype(BF)
    at, dt = AT[:, rows], DT[:, rows]
    _, n, rows_of, _ = GU.shape
    half = rows_of // 2
    dwt = mm(dt, act)
    dwg = mm(at, dgate).reshape(n, half, COLS)
    dwu = mm(at, dup).reshape(n, half, COLS)
    if t == 0:
        DWT[...] = dwt
        GU[slot, :, :half, :] = dwg
        GU[slot, :, half:, :] = dwu
    else:
        DWT[...] += dwt
        GU[slot, :, :half, :] += dwg
        GU[slot, :, half:, :] += dwu
    if top:
        da = mm_nt(dgate, wg) + mm_nt(dup, wu)

        S[rows, :] += da


def through_norm(rows, A, D, DT, S):
    h = A[rows, :].astype(F32)
    s = lax.rsqrt(jnp.mean(h * h, -1, keepdims=True) + 1e-6)
    da = S[rows, :].astype(BF).astype(F32)
    dh = da * s - h * (s * s * s * jnp.mean(da * h, -1, keepdims=True))
    dh = (D[rows, :].astype(F32) + dh.astype(BF).astype(F32)).astype(BF)
    D[rows, :] = dh
    DT[:, rows] = dh.T


def adamw(w, m, v, g):
    m = 0.9 * m + 0.1 * g
    v = 0.95 * v + 0.05 * g * g
    step = m * lax.rsqrt(v + 1e-8) + 0.1 * w
    return (w - 0.02 * step).astype(BF), m, v


class Ring:
    def __init__(self, n, me, got, sems):
        self.n, self.me, self.hops = n, me, n // 2
        self.to = (lax.rem(me + n - 1, n), lax.rem(me + 1, n))
        self.got = got
        self.sum_out, self.sum_in, self.new_out, self.new_in = sems

    def owner(self, way, distance):
        return lax.rem(self.me + (self.n - distance if way == 0 else distance), self.n)

    def part(self, way, half_only):
        rows = self.got.shape[2]
        if not half_only:
            return slice(0, rows)
        return slice(0, rows // 2) if way == 0 else slice(rows // 2, rows)

    def sum_copy(self, way, step):
        part = self.part(way, step == 0)
        source = self.got.at[way, self.hops - 1, part] if step == 0 else self.got.at[way, step - 1]
        return pltpu.make_async_remote_copy(
            source, self.got.at[way, step, part], self.sum_out.at[way, step], self.sum_in.at[way, step],
            device_id={"dp": self.to[way]}, device_id_type=MESH,
        )

    def new_copy(self, way, step, new):
        part = self.part(way, step == self.hops - 1)
        block = new.at[self.owner(1 - way, step), part]
        return pltpu.make_async_remote_copy(
            block, block, self.new_out.at[way, step], self.new_in.at[way, step],
            device_id={"dp": self.to[way]}, device_id_type=MESH,
        )

    def arrived(self, way, step, new):
        part = self.part(way, step == self.hops - 1)
        block = new.at[self.owner(1 - way, step + 1), part]
        return pltpu.make_async_remote_copy(
            block, block, self.new_out.at[way, step], self.new_in.at[way, step],
            device_id={"dp": self.to[way]}, device_id_type=MESH,
        )

    def sum_step(self, step, local):
        for way in (0, 1):
            if step:
                before = self.sum_copy(way, step - 1)
                before.wait_send()
                before.wait_recv()
        for way in (0, 1):
            term = local(self.owner(way, self.hops - step))
            if step == 0:
                self.got[way, self.hops - 1, self.part(way, True)] = term[self.part(way, True)].astype(BF)
            elif step == 1:
                mine, other = self.part(way, True), self.part(1 - way, True)
                got = self.got[way, 0, mine].astype(F32)
                self.got[way, 0, mine] = (got + term[mine]).astype(BF)
                self.got[way, 0, other] = term[other].astype(BF)
            else:
                self.got[way, step - 1] = (self.got[way, step - 1].astype(F32) + term).astype(BF)
        for way in (0, 1):
            self.sum_copy(way, step).start()

    def total(self, local):
        for way in (0, 1):
            before = self.sum_copy(way, self.hops - 1)
            before.wait_send()
            before.wait_recv()
        total = local(self.me) + self.got[0, self.hops - 1].astype(F32) + self.got[1, self.hops - 1].astype(F32)
        return total.astype(BF).astype(F32)

    def new_step(self, step, new):
        for way in (0, 1):
            if step:
                self.new_copy(way, step - 1, new).wait_send()
                self.arrived(way, step - 1, new).wait_recv()
        if step < self.hops:
            for way in (0, 1):
                self.new_copy(way, step, new).start()


def grads_kernel(
    n, dy_h, a1_h, a1t_h, a2_h, a2t_h, h_h, dyt_h, wg_h, wu_h, wd_h, mg_h, mu_h, md_h, vg_h, vu_h, vd_h,
    wg_o, wu_o, wd_o, mg_o, mu_o, md_o, vg_o, vu_o, vd_o,
    A, AT, D, DT, S, WG, WU, WD, GU, DWT, NEW, NEWD, GOT, GOTD, MV, MVD,
    load, wsem, hsem, ring_sem, ringd_sem, mv_in, mv_out, mvd_in, mvd_out, out_sem, outd_sem,
):
    me = lax.axis_index("dp")
    left, right = lax.rem(me + n - 1, n), lax.rem(me + 1, n)
    barrier = pltpu.get_barrier_semaphore()
    for neighbour in (left, right):
        pl.semaphore_signal(barrier, inc=1, device_id={"dp": neighbour}, device_id_type=MESH)

    tokens, d = A.shape
    nt = tokens // TOK
    ff = WG.shape[2]
    nj = ff // COLS
    half, down = d // n, ff // n
    hops = n // 2
    streams = d // WIDE

    def tile_loads(t, a_h, at_h, with_dy):
        rows = slice(t * TOK, (t + 1) * TOK)
        pairs = [(a_h.at[rows, :], A.at[rows, :]), (at_h.at[:, rows], AT.at[:, rows])]
        if with_dy:
            pairs += [(dy_h.at[0, rows, :], D.at[rows, :]), (dyt_h.at[:, rows], DT.at[:, rows])]
        return [pltpu.make_async_copy(s, o, load.at[t, i]) for i, (s, o) in enumerate(pairs)]

    def h_load(t):
        rows = slice(t * TOK, (t + 1) * TOK)
        return pltpu.make_async_copy(h_h.at[rows, :], A.at[rows, :], hsem.at[t])

    weights = [
        pltpu.make_async_copy(s.at[l], o.at[l], wsem.at[l, i])
        for l in (1, 0) for i, (s, o) in enumerate(((wg_h, WG), (wu_h, WU), (wd_h, WD)))
    ]
    for c in weights[:3]:
        c.start()
    for t in range(nt):
        for c in tile_loads(t, a2_h, a2t_h, True):
            c.start()
    for c in weights[3:]:
        c.start()
    S[:tokens, :] = jnp.zeros((tokens, d), F32)
    for c in weights[:3]:
        c.wait()
    pl.semaphore_wait(barrier, 2)

    refs = (A, AT, D, DT, S, WG, WU, WD, GU, DWT)

    def gate_up(c, op, step):
        slot, layer, j = lax.rem(c, SLOTS), 1 - c // nj, lax.rem(c, nj)
        ring = Ring(n, me, GOT.at[slot], [ring_sem.at[k, slot] for k in range(4)])
        new = NEW.at[c]
        cols = pl.ds(pl.multiple_of(j * COLS, COLS), COLS)
        place = lax.rem(c, 2)

        def local(device):
            return GU[slot, device]

        def moments(m_g, m_u, v_g, v_u):
            return [
                (m_g.at[layer, :, cols], MV.at[place, 0, :half]), (m_u.at[layer, :, cols], MV.at[place, 0, half:]),
                (v_g.at[layer, :, cols], MV.at[place, 1, :half]), (v_u.at[layer, :, cols], MV.at[place, 1, half:]),
            ]

        fetch = lambda: [pltpu.make_async_copy(a, b, mv_in.at[place, i]) for i, (a, b) in enumerate(moments(mg_h, mu_h, vg_h, vu_h))]
        keep = lambda: [pltpu.make_async_copy(b, a, mv_out.at[place, i]) for i, (a, b) in enumerate(moments(mg_o, mu_o, vg_o, vu_o))]
        write = lambda: [
            pltpu.make_async_copy(new.at[:, :half], wg_o.at[layer, :, :, cols], out_sem.at[place, 0]),
            pltpu.make_async_copy(new.at[:, half:], wu_o.at[layer, :, :, cols], out_sem.at[place, 1]),
        ]
        if op == "sum":
            if step == hops // 2:
                @pl.when(c >= 2)
                def _():
                    for copy in keep():
                        copy.wait()
                for copy in fetch():
                    copy.start()
            ring.sum_step(step, local)
        elif op == "update":
            for copy in fetch():
                copy.wait()
            g = ring.total(local)
            own = pl.ds(pl.multiple_of(me * half, half), half)
            for i, w in enumerate((WG, WU)):
                rows = slice(i * half, (i + 1) * half)
                nw, m, v = adamw(w[layer, own, cols].astype(F32), MV[place, 0, rows], MV[place, 1, rows], g[rows])
                MV[place, 0, rows] = m
                MV[place, 1, rows] = v
                NEW[c, me, rows] = nw
            ring.new_step(0, new)
            for copy in keep():
                copy.start()
        else:
            ring.new_step(step, new)
            if step == hops:
                @pl.when(c >= 2)
                def _():
                    for copy in write():
                        copy.wait()
                for copy in write():
                    copy.start()

    def down_block(layer, k, op, step):
        ring = Ring(n, me, GOTD.at[k], [ringd_sem.at[i, k] for i in range(4)])
        new = NEWD.at[layer, k]
        cols = slice(k * WIDE, (k + 1) * WIDE)

        def local(device):
            return S[pl.ds(pl.multiple_of(layer * tokens + device * down, 32), down), cols]

        fetch = lambda: [pltpu.make_async_copy(s.at[layer, :, cols], MVD.at[k, i], mvd_in.at[k, i]) for i, s in enumerate((md_h, vd_h))]
        keep = lambda: [pltpu.make_async_copy(MVD.at[k, i], o.at[layer, :, cols], mvd_out.at[k, i]) for i, o in enumerate((md_o, vd_o))]
        write = lambda: pltpu.make_async_copy(new, wd_o.at[layer, :, :, cols], outd_sem.at[k])
        if op == "sum":
            if step == hops // 2:
                @pl.when(layer == 0)
                def _():
                    for copy in keep():
                        copy.wait()
                for copy in fetch():
                    copy.start()
            ring.sum_step(step, local)
        elif op == "update":
            for copy in fetch():
                copy.wait()
            g = ring.total(local)
            own = pl.ds(pl.multiple_of(me * down, 32), down)
            nw, m, v = adamw(WD[layer, own, cols].astype(F32), MVD[k, 0], MVD[k, 1], g)
            MVD[k, 0] = m
            MVD[k, 1] = v
            NEWD[layer, k, me] = nw
            ring.new_step(0, new)
            for copy in keep():
                copy.start()
        else:
            ring.new_step(step, new)
            if step == hops:
                @pl.when(layer == 0)
                def _():
                    write().wait()
                write().start()

    steps = [("sum", s, 2 * s) for s in range(hops)] + [("update", 0, 2 * hops)]
    steps += [("new", s, 2 * hops + 1 + 2 * s) for s in range(1, hops + 1)]

    def tick(i, t, with_down):
        for op, step, after in steps:
            ago, at_tick = divmod(after, nt)
            if at_tick == t:
                c = i - 1 - ago

                @pl.when((c >= 0) & (c < 2 * nj))
                def _(c=c, op=op, step=step):
                    gate_up(c, op, step)
        if with_down:
            for k in range(streams):
                for op, step, after in steps:
                    ago, at_tick = divmod(after + 1 + 2 * k, nt)
                    if at_tick == t:
                        ready = i - ago

                        @pl.when((ready == nj) | (ready == 2 * nj))
                        def _(ready=ready, op=op, step=step, k=k):
                            down_block(2 - ready // nj, k, op, step)

    def finish(layer, j):
        S[pl.ds(pl.multiple_of(layer * tokens + j * COLS, COLS), COLS), :] = DWT[...].T

    def top_block(j, carry):
        for t in range(nt):
            tick(j, t, False)

            @pl.when(j == 0)
            def _():
                for c in tile_loads(t, a2_h, a2t_h, True):
                    c.wait()
            tile_grads(True, 1, j, t, lax.rem(j, SLOTS), refs)

            @pl.when(j == nj - 1)
            def _():
                h_load(t).start()
                tile_loads(t, a1_h, a1t_h, False)[1].start()
        finish(1, j)
        return carry

    lax.fori_loop(0, nj, top_block, 0)
    for c in weights[3:]:
        c.wait()
    for t in range(nt):
        h_load(t).wait()
        for u in range(TOK // TILE):
            through_norm(slice(t * TOK + u * TILE, t * TOK + (u + 1) * TILE), A, D, DT, S)
        tile_loads(t, a1_h, a1t_h, False)[0].start()

    def low_block(i, carry):
        for t in range(nt):
            tick(i, t, True)

            @pl.when(i < 2 * nj)
            def _():
                @pl.when(i == nj)
                def _():
                    for c in tile_loads(t, a1_h, a1t_h, False):
                        c.wait()
                tile_grads(False, 0, i - nj, t, lax.rem(i, SLOTS), refs)

        @pl.when(i < 2 * nj)
        def _():
            finish(0, i - nj)
        return carry

    last = 2 * nj + max(nt + steps[-1][2], 1 + 2 * (streams - 1) + steps[-1][2]) // nt
    lax.fori_loop(nj, last + 1, low_block, 0)

    for c in (2 * nj - 2, 2 * nj - 1):
        place, j = c % 2, c % nj
        cols = slice(j * COLS, (j + 1) * COLS)
        for i, o in enumerate((mg_o, mu_o, vg_o, vu_o)):
            pltpu.make_async_copy(MV.at[place, i // 2, (i % 2) * half : (i % 2 + 1) * half], o.at[0, :, cols], mv_out.at[place, i]).wait()
        for i, o in enumerate((wg_o, wu_o)):
            pltpu.make_async_copy(NEW.at[c, :, i * half : (i + 1) * half], o.at[0, :, :, cols], out_sem.at[place, i]).wait()
    for k in range(streams):
        cols = slice(k * WIDE, (k + 1) * WIDE)
        for i, o in enumerate((md_o, vd_o)):
            pltpu.make_async_copy(MVD.at[k, i], o.at[0, :, cols], mvd_out.at[k, i]).wait()
        pltpu.make_async_copy(NEWD.at[0, k], wd_o.at[0, :, :, cols], outd_sem.at[k]).wait()


def grads(n, *args):
    a1, wg, wd = args[1], args[7], args[9]
    tokens, d = a1.shape
    layers, _, ff = wg.shape
    nj, nt, hops, streams = ff // COLS, tokens // TOK, n // 2, d // WIDE
    half, down = d // n, ff // n
    any_ = pl.BlockSpec(memory_space=pl.ANY)
    dma = pltpu.SemaphoreType.DMA
    own = [jax.ShapeDtypeStruct((layers, half, ff), F32)] * 2 + [jax.ShapeDtypeStruct((layers, down, d), F32)]
    return pl.pallas_call(
        functools.partial(grads_kernel, n),
        in_specs=[any_] * len(args),
        out_specs=[any_] * 9,
        out_shape=[jax.ShapeDtypeStruct((layers, n, half, ff), BF)] * 2 + [jax.ShapeDtypeStruct((layers, n, down, d), BF)] + own + own,
        scratch_shapes=[
            pltpu.VMEM((tokens, d), BF), pltpu.VMEM((d, tokens), BF), pltpu.VMEM((tokens, d), BF), pltpu.VMEM((d, tokens), BF),
            pltpu.VMEM((tokens + ff, d), F32),
            pltpu.VMEM((layers, d, ff), BF), pltpu.VMEM((layers, d, ff), BF), pltpu.VMEM((layers, ff, d), BF),
            pltpu.VMEM((SLOTS, n, 2 * half, COLS), F32), pltpu.VMEM((d, COLS), F32),
            pltpu.VMEM((layers * nj, n, 2 * half, COLS), BF), pltpu.VMEM((layers, streams, n, down, WIDE), BF),
            pltpu.VMEM((SLOTS, 2, hops, 2 * half, COLS), BF),
            pltpu.VMEM((streams, 2, hops, down, WIDE), BF),
            pltpu.VMEM((2, 2, 2 * half, COLS), F32), pltpu.VMEM((streams, 2, down, WIDE), F32),
            dma((nt, 4)), dma((2, 3)), dma((nt,)), dma((4, SLOTS, 2, hops)), dma((4, streams, 2, hops)),
            dma((2, 4)), dma((2, 4)), dma((streams, 2)), dma((streams, 2)), dma((2, 2)), dma((streams,)),
        ],
        compiler_params=pltpu.CompilerParams(vmem_limit_bytes=VMEM_LIMIT, collective_id=0, has_side_effects=True),
        name="grads",
    )(*args)


def solution(mesh):
    n = mesh.shape["dp"]

    def step(x, dy, wg, wu, wd, mg, mu, md, vg, vu, vd):
        a1, a1t, a2, a2t, h, dyt = forward(x, dy, wg, wu, wd)
        out = grads(n, dy, a1, a1t, a2, a2t, h, dyt, wg, wu, wd, mg, mu, md, vg, vu, vd)
        return tuple(t.reshape(t.shape[0], -1, t.shape[-1]) for t in out)

    data, whole, own = P(("rep", "dp"), None, None), P(), P(None, "dp", None)
    return jax.shard_map(
        step, mesh=mesh, in_specs=(data,) * 2 + (whole,) * 3 + (own,) * 6,
        out_specs=(P("rep", None, None),) * 3 + (P("rep", "dp", None),) * 6, check_vma=False,
    )
```

time: 599 us -> 308 us (0.51)
  waiting for transfers between devices: 358 us -> 0 us
  Pallas kernels: 173 us -> 292 us
  other arithmetic: 26.4 us -> 0 us
  between operations: 14.4 us -> 0.67 us
  local copies, waits for them, and re-layouts: 26.5 us -> 15.1 us
    all_gather x6 -> x0, waiting for transfers between devices: 196 us -> none  [step(): new[l, k] = (lax.all_gather(nw, 'dp', axis=0, tiled=True), nm, nv)]
    reduce_scatter x4 -> x0, waiting for transfers between devices: 158 us -> none  [the longest x2 88.9 us: step(): gul = lax.psum_scatter(gu[l], 'dp', scatter_dimension=0, tiled=True)]
    pallas_call x1, Pallas kernels: 141 us -> 260 us  [grads(): pl.pallas_call(functools.partial(grads_kernel, n), in_specs=[any_] * len(...]
    another operation x6 -> x0, other arithmetic: 18.1 us -> none  [step(): jnp.stack([new[l, k][which] for l in range(layers)])]
    unnamed x18 -> x25, local copies, waits for them, and re-layouts: 0.61 us -> 15.1 us
    slice x9 -> x0, local copies, waits for them, and re-layouts: 11.7 us -> none  [the longest x3 10.2 us: step(): w[l]]
    squeeze x2 -> x0, local copies, waits for them, and re-layouts: 11.4 us -> none  [the longest x1 7.15 us: step(): gul = lax.psum_scatter(gu[l], 'dp', scatter_dimension=0, tiled=True)]
    convert_element_type x3 -> x0, other arithmetic: 6.4 us -> none  [adamw(): return ((w - 0.02 * step).astype(BF), m, v)]
  transfers between devices with their start and end apart: 10 -> 0, of which waited for: 10 -> 0; matrix products, arithmetic and copies ran while one was open for 7% -> 0% of each run, Pallas kernels for 0% -> 0%
where the time goes in v2:
time: 308 us
  Pallas kernels  292 us (95%)
  local copies, waits for them, and re-layouts  15.1 us (5%)
    pallas_call x1, Pallas kernels, grads(): pl.pallas_call(functools.partial(grads_kernel, n), in_specs=[any_] * len(...  260 us
    pallas_call x1, Pallas kernels, forward(): pl.pallas_call(forward_kernel, grid=(tokens // TILE,), in_specs=[row, row...  31.9 us
    unnamed x25, local copies, waits for them, and re-layouts  15.1 us

profile of v2, /device:TPU:22, one launch (start us, length us, event | category | flops | bytes accessed | tf_op | source)
XLA Modules:
  0.0 307.9 jit_solution(26889864825546108)
XLA Ops:
  0.6 31.9 %forward.1 = (bf16[4096,512]{1,0:T(8,128)(2,1)}, bf16[512,4096]{1,0:T(8,128)(2,1)}, bf16[4096,512]{1,0:T(8,128)(2,1)}, bf16[512,4096]{1,0:T(8,128)(2,1)}, bf16[4...) custom-call(bf16[1,4096,512]{2,1,0:T(8,128)(2,1)} %x_ref.1, bf16[1,4096,512]{2,1,0:T(8,128)(2,1)} %dy_h.1, ...), custom_call_target="tpu_custom_call" | custom-call | tf_op jit(solution)/shard_map/forward/pallas_call | solution.py:65
  32.6 260.2 %grads.1 = (bf16[2,8,64,1792]{3,2,1,0:T(8,128)(2,1)}, bf16[2,8,64,1792]{3,2,1,0:T(8,128)(2,1)}, bf16[2,8,224,512]{3,2,1,0:T(8,128)(2,1)}, f32[2,64,1792]{2,1,0:T...) custom-call(bf16[1,4096,512]{2,1,0:T(8,128)(2,1)} %dy_h.1, ...), custom_call_target="tpu_custom_call" | custom-call | tf_op jit(solution)/shard_map/grads/pallas_call | solution.py:443
  292.8 0.0 copy-start.1
  292.9 4.3 %copy.29 = bf16[2,512,1792]{2,1,0:T(8,128)(2,1)} copy(bf16[2,512,1792]{2,1,0:T(8,128)(2,1)} %bitcast.5) | data formatting | bytes 7340032
  297.1 0.0 copy-done.1
  297.1 0.0 copy-start
  297.1 1.9 copy.30
  299.0 1.5 copy-done
  300.5 0.0 copy-start.7
  300.5 0.0 copy-start.6
  300.5 1.9 copy.31
  302.4 0.0 copy-done.7
  302.4 0.0 copy-start.5
  302.4 0.0 copy-start.4
  302.4 0.0 copy-start.3
  302.4 0.9 copy.32
  303.3 0.0 copy-done.6
  303.3 0.0 copy-start.2
  303.3 0.9 copy.33
  304.2 0.0 copy-done.5
  304.2 0.9 copy.34
  305.1 0.0 copy-done.4
  305.1 0.9 copy.35
  306.1 0.0 copy-done.3
  306.1 0.9 copy.36
  307.0 0.0 copy-done.2
  307.0 0.9 copy.37
Async XLA Ops:
  292.8 4.3 %copy-start.1 = (bf16[2,8,64,1792]{3,2,1,0:T(8,128)(2,1)S(1)}, bf16[2,8,64,1792]{3,2,1,0:T(8,128)(2,1)}, u32[]{:S(2)}) copy-start(bf16[2,8,64,1792]{3,2,1,0:T(8,128)(2,1)} %get-tuple-element.31) | copy-start | bytes 11010052
  297.1 3.4 %copy-start = (bf16[2,8,224,512]{3,2,1,0:T(8,128)(2,1)S(1)}, bf16[2,8,224,512]{3,2,1,0:T(8,128)(2,1)}, u32[]{:S(2)}) copy-start(bf16[2,8,224,512]{3,2,1,0:T(8,128)(2,1)} %get-tuple-element.32) | copy-start | bytes 11010052
  300.5 1.9 copy-start.7
  300.5 2.8 copy-start.6
  302.4 1.9 copy-start.5
  302.4 2.8 copy-start.4
  302.4 3.7 %copy-start.3 = (f32[2,64,1792]{2,1,0:T(8,128)S(1)}, f32[2,64,1792]{2,1,0:T(8,128)}, u32[]{:S(2)}) copy-start(f32[2,64,1792]{2,1,0:T(8,128)} %get-tuple-element.55) | copy-start | bytes 2752516
  303.3 3.7 %copy-start.2 = (f32[2,224,512]{2,1,0:T(8,128)S(1)}, f32[2,224,512]{2,1,0:T(8,128)}, u32[]{:S(2)}) copy-start(f32[2,224,512]{2,1,0:T(8,128)} %get-tuple-element.56) | copy-start | bytes 2752516

commit v3 on v2

--- a/solution.py
+++ b/solution.py
@@ -13,6 +13,8 @@
 TOK = 1024
 COLS = 256
 WIDE = 256
+DTOK = 256
+PAUSE = 2
 SLOTS = 3
 MESH = pl.DeviceIdType.MESH
 VMEM_LIMIT = 67043328
@@ -73,8 +75,8 @@
     )(x, dy, wg, wu, wd)
 
 
-def tile_grads(top, layer, j, t, slot, refs):
-    A, AT, D, DT, S, WG, WU, WD, GU, DWT = refs
+def tile_grads(layer, j, t, slot, refs, keep=None):
+    A, AT, D, DT, WG, WU, WD, GU, DWT = refs
     rows = slice(t * TOK, (t + 1) * TOK)
     cols = pl.ds(pl.multiple_of(j * COLS, COLS), COLS)
     wg, wu = WG[layer, :, cols], WU[layer, :, cols]
@@ -86,6 +88,9 @@
     act = (silu * up).astype(BF)
     dup = (dact * silu).astype(BF)
     dgate = (dact * up * (sig + silu * (1.0 - sig))).astype(BF)
+    if keep is not None:
+        keep[0] = dgate
+        keep[1] = dup
     at, dt = AT[:, rows], DT[:, rows]
     _, n, rows_of, _ = GU.shape
     half = rows_of // 2
@@ -100,16 +105,12 @@
         DWT[...] += dwt
         GU[slot, :, :half, :] += dwg
         GU[slot, :, half:, :] += dwu
-    if top:
-        da = mm_nt(dgate, wg) + mm_nt(dup, wu)
-
-        S[rows, :] += da
-
-
-def through_norm(rows, A, D, DT, S):
+
+
+def through_norm(rows, da, A, D, DT):
     h = A[rows, :].astype(F32)
     s = lax.rsqrt(jnp.mean(h * h, -1, keepdims=True) + 1e-6)
-    da = S[rows, :].astype(BF).astype(F32)
+    da = da.astype(BF).astype(F32)
     dh = da * s - h * (s * s * s * jnp.mean(da * h, -1, keepdims=True))
     dh = (D[rows, :].astype(F32) + dh.astype(BF).astype(F32)).astype(BF)
     D[rows, :] = dh
@@ -203,9 +204,9 @@
 
 def grads_kernel(
     n, dy_h, a1_h, a1t_h, a2_h, a2t_h, h_h, dyt_h, wg_h, wu_h, wd_h, mg_h, mu_h, md_h, vg_h, vu_h, vd_h,
-    wg_o, wu_o, wd_o, mg_o, mu_o, md_o, vg_o, vu_o, vd_o,
-    A, AT, D, DT, S, WG, WU, WD, GU, DWT, NEW, NEWD, GOT, GOTD, MV, MVD,
-    load, wsem, hsem, ring_sem, ringd_sem, mv_in, mv_out, mvd_in, mvd_out, out_sem, outd_sem,
+    wg_o, wu_o, wd_o, mg_o, mu_o, md_o, vg_o, vu_o, vd_o, dgu_h,
+    A, AT, D, DT, S, WG, WU, WD, GU, DWT, NEW, NEWD, GOT, GOTD, MV, MVD, OUT, IN,
+    load, wsem, hsem, ring_sem, ringd_sem, mv_in, mv_out, mvd_in, mvd_out, out_sem, outd_sem, dgu_out, dgu_in,
 ):
     me = lax.axis_index("dp")
     left, right = lax.rem(me + n - 1, n), lax.rem(me + 1, n)
@@ -238,17 +239,13 @@
     ]
     for c in weights[:3]:
         c.start()
-    for t in range(nt):
-        for c in tile_loads(t, a2_h, a2t_h, True):
-            c.start()
-    for c in weights[3:]:
+    for c in tile_loads(0, a2_h, a2t_h, True):
         c.start()
-    S[:tokens, :] = jnp.zeros((tokens, d), F32)
     for c in weights[:3]:
         c.wait()
     pl.semaphore_wait(barrier, 2)
 
-    refs = (A, AT, D, DT, S, WG, WU, WD, GU, DWT)
+    refs = (A, AT, D, DT, WG, WU, WD, GU, DWT)
 
     def gate_up(c, op, step):
         slot, layer, j = lax.rem(c, SLOTS), 1 - c // nj, lax.rem(c, nj)
@@ -311,7 +308,7 @@
         cols = slice(k * WIDE, (k + 1) * WIDE)
 
         def local(device):
-            return S[pl.ds(pl.multiple_of(layer * tokens + device * down, 32), down), cols]
+            return S[pl.ds(pl.multiple_of(layer * ff + device * down, 32), down), cols]
 
         fetch = lambda: [pltpu.make_async_copy(s.at[layer, :, cols], MVD.at[k, i], mvd_in.at[k, i]) for i, s in enumerate((md_h, vd_h))]
         keep = lambda: [pltpu.make_async_copy(MVD.at[k, i], o.at[layer, :, cols], mvd_out.at[k, i]) for i, o in enumerate((md_o, vd_o))]
@@ -352,11 +349,11 @@
         for op, step, after in steps:
             ago, at_tick = divmod(after, nt)
             if at_tick == t:
-                c = i - 1 - ago
-
-                @pl.when((c >= 0) & (c < 2 * nj))
-                def _(c=c, op=op, step=step):
-                    gate_up(c, op, step)
+                x = i - 1 - ago
+
+                @pl.when(((x >= 0) & (x < nj)) | ((x >= nj + PAUSE) & (x < 2 * nj + PAUSE)))
+                def _(x=x, op=op, step=step):
+                    gate_up(x - PAUSE * (x // (nj + PAUSE)), op, step)
         if with_down:
             for k in range(streams):
                 for op, step, after in steps:
@@ -364,12 +361,21 @@
                     if at_tick == t:
                         ready = i - ago
 
-                        @pl.when((ready == nj) | (ready == 2 * nj))
+                        @pl.when((ready == nj) | (ready == 2 * nj + PAUSE))
                         def _(ready=ready, op=op, step=step, k=k):
                             down_block(2 - ready // nj, k, op, step)
 
     def finish(layer, j):
-        S[pl.ds(pl.multiple_of(layer * tokens + j * COLS, COLS), COLS), :] = DWT[...].T
+        S[pl.ds(pl.multiple_of(layer * ff + j * COLS, COLS), COLS), :] = DWT[...].T
+
+    def dgu_write(j, t):
+        rows = slice(t * TOK, (t + 1) * TOK)
+        cols = pl.ds(pl.multiple_of(j * COLS, COLS), COLS)
+        return [pltpu.make_async_copy(OUT.at[t % 2, i], dgu_h.at[i, rows, cols], dgu_out.at[t % 2, i]) for i in (0, 1)]
+
+    def dgu_read(number, slot):
+        rows = pl.ds(pl.multiple_of(number * DTOK, DTOK), DTOK)
+        return [pltpu.make_async_copy(dgu_h.at[i, rows, :], IN.at[slot, i], dgu_in.at[slot, i]) for i in (0, 1)]
 
     def top_block(j, carry):
         for t in range(nt):
@@ -379,7 +385,20 @@
             def _():
                 for c in tile_loads(t, a2_h, a2t_h, True):
                     c.wait()
-            tile_grads(True, 1, j, t, lax.rem(j, SLOTS), refs)
+                if t + 1 < nt:
+                    for c in tile_loads(t + 1, a2_h, a2t_h, True):
+                        c.start()
+                else:
+                    for c in weights[3:]:
+                        c.start()
+
+            @pl.when((j > 0) | (t > 1))
+            def _():
+                for c in dgu_write(j, t):
+                    c.wait()
+            tile_grads(1, j, t, lax.rem(j, SLOTS), refs, OUT.at[t % 2])
+            for c in dgu_write(j, t):
+                c.start()
 
             @pl.when(j == nj - 1)
             def _():
@@ -389,32 +408,61 @@
         return carry
 
     lax.fori_loop(0, nj, top_block, 0)
+    for t in (nt - 2, nt - 1):
+        for c in dgu_write(nj - 1, t):
+            c.wait()
+    subs = tokens // DTOK // (PAUSE * nt)
+    for v in range(2):
+        for c in dgu_read(v, v):
+            c.start()
     for c in weights[3:]:
         c.wait()
     for t in range(nt):
         h_load(t).wait()
-        for u in range(TOK // TILE):
-            through_norm(slice(t * TOK + u * TILE, t * TOK + (u + 1) * TILE), A, D, DT, S)
-        tile_loads(t, a1_h, a1t_h, False)[0].start()
+
+    def between(i, t):
+        for v in range(subs):
+            number = ((i - nj) * nt + t) * subs + v
+            slot = v % 2
+            for c in dgu_read(number, slot):
+                c.wait()
+            da = mm_nt(IN[slot, 0], WG[1]) + mm_nt(IN[slot, 1], WU[1])
+            through_norm(pl.ds(pl.multiple_of(number * DTOK, DTOK), DTOK), da, A, D, DT)
+
+            @pl.when(number + 2 < tokens // DTOK)
+            def _(number=number, slot=slot):
+                for c in dgu_read(number + 2, slot):
+                    c.start()
 
     def low_block(i, carry):
+        low = i - nj - PAUSE
         for t in range(nt):
             tick(i, t, True)
 
-            @pl.when(i < 2 * nj)
+            @pl.when(low < 0)
             def _():
-                @pl.when(i == nj)
+                between(i, t)
+
+            @pl.when((low >= 0) & (low < nj))
+            def _():
+                @pl.when(low == 0)
                 def _():
                     for c in tile_loads(t, a1_h, a1t_h, False):
                         c.wait()
-                tile_grads(False, 0, i - nj, t, lax.rem(i, SLOTS), refs)
-
-        @pl.when(i < 2 * nj)
+                tile_grads(0, low, t, lax.rem(i - PAUSE, SLOTS), refs)
+
+        for p in range(PAUSE):
+            @pl.when(i == nj + p)
+            def _():
+                for t in range(p * nt // PAUSE, (p + 1) * nt // PAUSE):
+                    tile_loads(t, a1_h, a1t_h, False)[0].start()
+
+        @pl.when((low >= 0) & (low < nj))
         def _():
-            finish(0, i - nj)
+            finish(0, low)
         return carry
 
-    last = 2 * nj + max(nt + steps[-1][2], 1 + 2 * (streams - 1) + steps[-1][2]) // nt
+    last = 2 * nj + PAUSE + max(nt + steps[-1][2], 1 + 2 * (streams - 1) + steps[-1][2]) // nt
     lax.fori_loop(nj, last + 1, low_block, 0)
 
     for c in (2 * nj - 2, 2 * nj - 1):
@@ -443,23 +491,24 @@
     return pl.pallas_call(
         functools.partial(grads_kernel, n),
         in_specs=[any_] * len(args),
-        out_specs=[any_] * 9,
-        out_shape=[jax.ShapeDtypeStruct((layers, n, half, ff), BF)] * 2 + [jax.ShapeDtypeStruct((layers, n, down, d), BF)] + own + own,
+        out_specs=[any_] * 10,
+        out_shape=[jax.ShapeDtypeStruct((layers, n, half, ff), BF)] * 2 + [jax.ShapeDtypeStruct((layers, n, down, d), BF)] + own + own + [jax.ShapeDtypeStruct((2, tokens, ff), BF)],
         scratch_shapes=[
             pltpu.VMEM((tokens, d), BF), pltpu.VMEM((d, tokens), BF), pltpu.VMEM((tokens, d), BF), pltpu.VMEM((d, tokens), BF),
-            pltpu.VMEM((tokens + ff, d), F32),
+            pltpu.VMEM((layers * ff, d), F32),
             pltpu.VMEM((layers, d, ff), BF), pltpu.VMEM((layers, d, ff), BF), pltpu.VMEM((layers, ff, d), BF),
             pltpu.VMEM((SLOTS, n, 2 * half, COLS), F32), pltpu.VMEM((d, COLS), F32),
             pltpu.VMEM((layers * nj, n, 2 * half, COLS), BF), pltpu.VMEM((layers, streams, n, down, WIDE), BF),
             pltpu.VMEM((SLOTS, 2, hops, 2 * half, COLS), BF),
             pltpu.VMEM((streams, 2, hops, down, WIDE), BF),
             pltpu.VMEM((2, 2, 2 * half, COLS), F32), pltpu.VMEM((streams, 2, down, WIDE), F32),
+            pltpu.VMEM((2, 2, TOK, COLS), BF), pltpu.VMEM((2, 2, DTOK, ff), BF),
             dma((nt, 4)), dma((2, 3)), dma((nt,)), dma((4, SLOTS, 2, hops)), dma((4, streams, 2, hops)),
-            dma((2, 4)), dma((2, 4)), dma((streams, 2)), dma((streams, 2)), dma((2, 2)), dma((streams,)),
+            dma((2, 4)), dma((2, 4)), dma((streams, 2)), dma((streams, 2)), dma((2, 2)), dma((streams,)), dma((2, 2)), dma((2, 2)),
         ],
         compiler_params=pltpu.CompilerParams(vmem_limit_bytes=VMEM_LIMIT, collective_id=0, has_side_effects=True),
         name="grads",
-    )(*args)
+    )(*args)[:9]
 
 
 def solution(mesh):

time: 308 us -> 299 us (0.971)
  Pallas kernels: 292 us -> 283 us
    pallas_call x1, Pallas kernels: 260 us -> 251 us  [grads(): pl.pallas_call(functools.partial(grads_kernel, n), in_specs=[any_] * len(...]
where the time goes in v3:
time: 299 us
  Pallas kernels  283 us (95%)
  local copies, waits for them, and re-layouts  15.1 us (5%)
    pallas_call x1, Pallas kernels, grads(): pl.pallas_call(functools.partial(grads_kernel, n), in_specs=[any_] * len(...  251 us
    pallas_call x1, Pallas kernels, forward(): pl.pallas_call(forward_kernel, grid=(tokens // TILE,), in_specs=[row, row...  31.9 us
    unnamed x25, local copies, waits for them, and re-layouts  15.1 us

profile of v3, /device:TPU:22, one launch (start us, length us, event | category | flops | bytes accessed | tf_op | source)
XLA Modules:
  0.0 298.7 jit_solution(6580993182590841852)
XLA Ops:
  0.6 31.9 %forward.1 = (bf16[4096,512]{1,0:T(8,128)(2,1)}, bf16[512,4096]{1,0:T(8,128)(2,1)}, bf16[4096,512]{1,0:T(8,128)(2,1)}, bf16[512,4096]{1,0:T(8,128)(2,1)}, bf16[4...) custom-call(bf16[1,4096,512]{2,1,0:T(8,128)(2,1)} %x_ref.1, bf16[1,4096,512]{2,1,0:T(8,128)(2,1)} %dy_h.1, ...), custom_call_target="tpu_custom_call" | custom-call | tf_op jit(solution)/shard_map/forward/pallas_call | solution.py:67
  32.6 251.0 %grads.1 = (bf16[2,8,64,1792]{3,2,1,0:T(8,128)(2,1)}, bf16[2,8,64,1792]{3,2,1,0:T(8,128)(2,1)}, bf16[2,8,224,512]{3,2,1,0:T(8,128)(2,1)}, f32[2,64,1792]{2,1,0:T...) custom-call(bf16[1,4096,512]{2,1,0:T(8,128)(2,1)} %dy_h.1, ...), custom_call_target="tpu_custom_call" | custom-call | tf_op jit(solution)/shard_map/grads/pallas_call | solution.py:491
  283.6 0.0 copy-start.1
  283.6 4.3 %copy.29 = bf16[2,512,1792]{2,1,0:T(8,128)(2,1)} copy(bf16[2,512,1792]{2,1,0:T(8,128)(2,1)} %bitcast.5) | data formatting | bytes 7340032
  287.9 0.0 copy-done.1
  287.9 0.0 copy-start
  287.9 1.9 copy.30
  289.7 1.5 copy-done
  291.2 0.0 copy-start.7
  291.2 0.0 copy-start.6
  291.2 0.0 copy-start.5
  291.2 1.9 copy.31
  293.1 0.0 copy-done.7
  293.1 0.0 copy-start.4
  293.1 0.0 copy-start.3
  293.1 0.0 copy-start.2
  293.1 0.9 copy.32
  294.1 0.0 copy-done.6
  294.1 0.9 copy.33
  295.0 0.0 copy-done.5
  295.0 0.9 copy.34
  295.9 0.0 copy-done.4
  295.9 0.9 copy.35
  296.8 0.0 copy-done.3
  296.8 0.9 copy.36
  297.8 0.0 copy-done.2
  297.8 0.9 copy.37
Async XLA Ops:
  283.6 4.3 %copy-start.1 = (bf16[2,8,64,1792]{3,2,1,0:T(8,128)(2,1)S(1)}, bf16[2,8,64,1792]{3,2,1,0:T(8,128)(2,1)}, u32[]{:S(2)}) copy-start(bf16[2,8,64,1792]{3,2,1,0:T(8,128)(2,1)} %get-tuple-element.31) | copy-start | bytes 11010052
  287.9 3.4 %copy-start = (bf16[2,8,224,512]{3,2,1,0:T(8,128)(2,1)S(1)}, bf16[2,8,224,512]{3,2,1,0:T(8,128)(2,1)}, u32[]{:S(2)}) copy-start(bf16[2,8,224,512]{3,2,1,0:T(8,128)(2,1)} %get-tuple-element.32) | copy-start | bytes 11010052
  291.2 1.9 copy-start.7
  291.2 2.8 copy-start.6
  291.2 3.7 %copy-start.5 = (f32[2,224,512]{2,1,0:T(8,128)S(1)}, f32[2,224,512]{2,1,0:T(8,128)}, u32[]{:S(2)}) copy-start(f32[2,224,512]{2,1,0:T(8,128)} %get-tuple-element.53) | copy-start | bytes 2752516
  293.1 2.8 copy-start.4
  293.1 3.7 %copy-start.3 = (f32[2,64,1792]{2,1,0:T(8,128)S(1)}, f32[2,64,1792]{2,1,0:T(8,128)}, u32[]{:S(2)}) copy-start(f32[2,64,1792]{2,1,0:T(8,128)} %get-tuple-element.55) | copy-start | bytes 2752516
  293.1 4.6 %copy-start.2 = (f32[2,224,512]{2,1,0:T(8,128)S(1)}, f32[2,224,512]{2,1,0:T(8,128)}, u32[]{:S(2)}) copy-start(f32[2,224,512]{2,1,0:T(8,128)} %get-tuple-element.56) | copy-start | bytes 2752516

commit v4 on v3

--- a/solution.py
+++ b/solution.py
@@ -511,13 +511,41 @@
     )(*args)[:9]
 
 
+def place_kernel(count, *refs):
+    ins, outs, held, (arrive, leave) = refs[:count], refs[count : 2 * count], refs[2 * count : 3 * count], refs[3 * count :]
+    pieces = [(i, l) for i in range(count) for l in range(ins[i].shape[0])]
+    loads = [pltpu.make_async_copy(ins[i].at[l], held[i].at[l], arrive.at[i, l]) for i, l in pieces]
+    stores = [pltpu.make_async_copy(held[i].at[l], outs[i].at[l], leave.at[i, l]) for i, l in pieces]
+    for copy in loads:
+        copy.start()
+    for load, store in zip(loads, stores, strict=True):
+        load.wait()
+        store.start()
+    for store in stores:
+        store.wait()
+
+
+def place(arrays):
+    count, layers = len(arrays), arrays[0].shape[0]
+    any_ = pl.BlockSpec(memory_space=pl.ANY)
+    return pl.pallas_call(
+        functools.partial(place_kernel, count),
+        in_specs=[any_] * count,
+        out_specs=[any_] * count,
+        out_shape=[jax.ShapeDtypeStruct(t.shape, t.dtype) for t in arrays],
+        scratch_shapes=[pltpu.VMEM(t.shape, t.dtype) for t in arrays] + [pltpu.SemaphoreType.DMA((count, layers))] * 2,
+        compiler_params=pltpu.CompilerParams(vmem_limit_bytes=VMEM_LIMIT),
+        name="place",
+    )(*arrays)
+
+
 def solution(mesh):
     n = mesh.shape["dp"]
 
     def step(x, dy, wg, wu, wd, mg, mu, md, vg, vu, vd):
         a1, a1t, a2, a2t, h, dyt = forward(x, dy, wg, wu, wd)
         out = grads(n, dy, a1, a1t, a2, a2t, h, dyt, wg, wu, wd, mg, mu, md, vg, vu, vd)
-        return tuple(t.reshape(t.shape[0], -1, t.shape[-1]) for t in out)
+        return tuple(place([t.reshape(t.shape[0], -1, t.shape[-1]) for t in out]))
 
     data, whole, own = P(("rep", "dp"), None, None), P(), P(None, "dp", None)
     return jax.shard_map(

time: 299 us -> 296 us (0.990)
  local copies, waits for them, and re-layouts: 15.1 us -> 0 us
  Pallas kernels: 283 us -> 295 us
    unnamed x25 -> x0, local copies, waits for them, and re-layouts: 15.1 us -> none
    pallas_call x0 -> x1, Pallas kernels: none -> 12.2 us  [place(): pl.pallas_call(functools.partial(place_kernel, count), in_specs=[any_] *...]
where the time goes in v4:
time: 296 us
  Pallas kernels  295 us (100%)
    pallas_call x1, Pallas kernels, grads(): pl.pallas_call(functools.partial(grads_kernel, n), in_specs=[any_] * len(...  251 us
    pallas_call x1, Pallas kernels, forward(): pl.pallas_call(forward_kernel, grid=(tokens // TILE,), in_specs=[row, row...  31.9 us
    pallas_call x1, Pallas kernels, place(): pl.pallas_call(functools.partial(place_kernel, count), in_specs=[any_] *...  12.2 us

profile of v4, /device:TPU:22, one launch (start us, length us, event | category | flops | bytes accessed | tf_op | source)
XLA Modules:
  0.0 296.1 jit_solution(16935073662118798708)
XLA Ops:
  0.6 31.9 %forward.1 = (bf16[4096,512]{1,0:T(8,128)(2,1)}, bf16[512,4096]{1,0:T(8,128)(2,1)}, bf16[4096,512]{1,0:T(8,128)(2,1)}, bf16[512,4096]{1,0:T(8,128)(2,1)}, bf16[4...) custom-call(bf16[1,4096,512]{2,1,0:T(8,128)(2,1)} %x_ref.1, bf16[1,4096,512]{2,1,0:T(8,128)(2,1)} %dy_h.1, ...), custom_call_target="tpu_custom_call" | custom-call | tf_op jit(solution)/shard_map/forward/pallas_call | solution.py:67
  32.6 251.2 %grads.1 = (bf16[2,8,64,1792]{3,2,1,0:T(8,128)(2,1)}, bf16[2,8,64,1792]{3,2,1,0:T(8,128)(2,1)}, bf16[2,8,224,512]{3,2,1,0:T(8,128)(2,1)}, f32[2,64,1792]{2,1,0:T...) custom-call(bf16[1,4096,512]{2,1,0:T(8,128)(2,1)} %dy_h.1, ...), custom_call_target="tpu_custom_call" | custom-call | tf_op jit(solution)/shard_map/grads/pallas_call | solution.py:491
  283.8 12.2 %place.1 = (bf16[2,512,1792]{2,1,0:T(8,128)(2,1)}, bf16[2,512,1792]{2,1,0:T(8,128)(2,1)}, bf16[2,1792,512]{2,1,0:T(8,128)(2,1)}, f32[2,64,1792]{2,1,0:T(8,128)},...) custom-call(bf16[2,512,1792]{2,1,0:T(8,128)(2,1)} %bitcast.3, ...), custom_call_target="tpu_custom_call" | custom-call | tf_op jit(solution)/shard_map/place/pallas_call | solution.py:531
